TPU v7x, 32 devices: a whole 2x2x4 slice. The times are simulated.
32 devices in a mesh: pass: 8 (over z, x), cell: 4 (over y, core).
Axes of the slice: x: 2, y: 2, z: 4, core: 2. Of those that a mesh axis runs over, the one named last changes fastest.
Arguments:
- flow_state: float32 [2048, 4096], P('pass', 'cell'), may hold values from -6 to 6
- face_weights: float32 [4, 2048, 4096], P(None, 'pass', 'cell'), may hold values from 0.02 to 0.24
- forcing: float32 [2048, 4096], P('pass', 'cell'), may hold values from -1.2 to 1.2
- lagged_planes: float32 [8, 8, 4096], P('pass', None, 'cell'), may hold values from -6 to 6
- phase_lag: int32 [4, 2], replicated, may hold values from 0 to 8
- face_map: int32 [8, 4096], P('pass', 'cell'), may hold values from 0 to 4095, as said below
- surface_record: bfloat16 [8, 120, 4096], P('pass', None, 'cell'), may hold values from -6 to 6
- face_radius: float32 [2, 4096], P(None, 'cell'), may hold values from 0.3 to 1
- face_angle: float32 [2, 4096], P(None, 'cell'), may hold values from -0.3 to 0.3
- face_axial: float32 [2, 4096], P(None, 'cell'), may hold values from -0.3 to 0.3
- face_stagger: float32 [2, 4096], P(None, 'cell'), may hold values from -1.2 to 1.2
- face_area: float32 [2, 4096], P(None, 'cell'), may hold values from 0.5 to 1.5
- listeners: float32 [3, 1024], replicated, as said below
- observer_group: int32 [1024], replicated, may hold values from 0 to 15
Outputs:
- final_field: float32 [2048, 4096], P('pass', 'cell')
- acoustic: float32 [1024, 128], P('cell')
- array_signal: float32 [16, 128], replicated
Inputs may be any that keep to these rules, and one draw needn't show every extreme that they name: face_map[j, a] lies in the aligned block of 1024 axial indices that holds a, and for each j the entries of a block are a permutation of that block. `listeners`: every observer is between 1.3 and 4 from the anchor.
All inputs are finite; a program needn't handle non-finite values.
Results may differ from a plain program's by a relative error of at most 0.0035.
Values sent between devices are 32-bit elements; how exact they have to be, the bound alone decides.
A program may use at most 64 MiB of HBM per device.

v0:
```python
import math
import jax
import jax.numpy as jnp
from jax import lax
from jax.sharding import PartitionSpec as P

STEPS = 8
GROUPS = 16
sound_speed = 2.0


def padded(shard, sides, width):
    for axis, dim in sides:
        devices, length = (lax.axis_size(axis), shard.shape[dim])
        up = [(i, (i + 1) % devices) for i in range(devices - 1)]
        down = [(j, i) for i, j in up]
        last = lax.slice_in_dim(shard, length - width, length, axis=dim)
        initial = lax.slice_in_dim(shard, 0, width, axis=dim)
        before = lax.ppermute(last, axis, up)
        after = lax.ppermute(initial, axis, down)
        shard = jnp.concatenate([before, shard, after], axis=dim)
    return shard


def shifted(block, axis, distance):
    devices = range(lax.axis_size(axis))
    route = [((i - distance) % len(devices), i) for i in devices]
    return lax.ppermute(block, axis, route)


def relax(field, coeff, forcing, ghost_low, ghost_high):
    edges = jnp.stack([field[:, 0], field[:, -1]], axis=0)
    rim = padded(edges, (("cell", 0),), 1)
    below = jnp.concatenate([ghost_low[None, :], field[:-1, :]], axis=0)
    above = jnp.concatenate([field[1:, :], ghost_high[None, :]], axis=0)
    left = jnp.concatenate([rim[0][:, None], field[:, :-1]], axis=1)
    right = jnp.concatenate([field[:, 1:], rim[3][:, None]], axis=1)
    keep = 1.0 - coeff[0] - coeff[1] - coeff[2] - coeff[3]
    return (
        keep * field
        + coeff[0] * below
        + coeff[1] * above
        + coeff[2] * left
        + coeff[3] * right
        + forcing
    )


def time_rate(signal, axis):
    values = signal.astype(jnp.float32)
    length = values.shape[axis]
    inner = (
        lax.slice_in_dim(values, 2, length, axis=axis)
        - lax.slice_in_dim(values, 0, length - 2, axis=axis)
    ) * 0.5
    head = lax.slice_in_dim(values, 1, 2, axis=axis) - lax.slice_in_dim(values, 0, 1, axis=axis)
    tail = lax.slice_in_dim(values, length - 1, length, axis=axis) - lax.slice_in_dim(
        values, length - 2, length - 1, axis=axis
    )
    return jnp.concatenate([head, inner, tail], axis=axis).astype(jnp.bfloat16)


def kernel_pair(points, theta, radius, angle, axial, stagger, area, scale):
    phase = theta + angle
    cos_phase = jnp.cos(phase)
    sin_phase = jnp.sin(phase)
    normal_x = -jnp.cos(stagger) * sin_phase
    normal_y = jnp.cos(stagger) * cos_phase
    normal_z = jnp.sin(stagger)
    delta_x = points[0][:, None] - (radius * cos_phase)[None, :]
    delta_y = points[1][:, None] - (radius * sin_phase)[None, :]
    delta_z = points[2][:, None] - axial[None, :]
    dist_sq = delta_x * delta_x + delta_y * delta_y + delta_z * delta_z
    dist = jnp.sqrt(dist_sq)
    cosine = (
        normal_x[None, :] * delta_x + normal_y[None, :] * delta_y + normal_z[None, :] * delta_z
    ) / dist
    weight = (area * scale / (4.0 * math.pi))[None, :] * cosine
    press = (weight / dist_sq).astype(jnp.bfloat16)
    change = (weight / (sound_speed * dist)).astype(jnp.bfloat16)
    return jnp.concatenate([press, change], axis=1)


def on_device(
    flow_state,
    face_weights,
    forcing,
    lagged_planes,
    phase_lag,
    face_map,
    surface_record,
    face_radius,
    face_angle,
    face_axial,
    face_stagger,
    face_area,
    listeners,
    observer_group,
):
    passes = lax.axis_size("pass")
    cells = lax.axis_size("cell")
    pass_index = lax.axis_index("pass")
    cell_index = lax.axis_index("cell")
    passage_count = passes // 2
    half = pass_index % 2
    passage = pass_index // 2
    field = flow_state
    height = field.shape[0]
    width = field.shape[1]
    lower_levels = jnp.concatenate([field[None, 0, :], lagged_planes[0]], axis=0)
    upper_levels = jnp.concatenate([field[None, -1, :], lagged_planes[0]], axis=0)
    local_map = face_map[0] - cell_index * width
    after_lag = phase_lag[(passage + 1) % passage_count, 0]
    before_lag = phase_lag[(passage + passage_count - 1) % passage_count, 1]
    surfaces = []
    for level in range(STEPS):
        up_pick = jnp.where(half == 1, after_lag, 0)
        down_pick = jnp.where(half == 0, before_lag, 0)
        raw_low = shifted(upper_levels[up_pick], "pass", 1)
        raw_high = shifted(lower_levels[down_pick], "pass", -1)
        mapped = jnp.take(jnp.where(half == 0, raw_low, raw_high), local_map)
        ghost_low = jnp.where(half == 0, mapped, raw_low)
        ghost_high = jnp.where(half == 1, mapped, raw_high)
        field = relax(field, face_weights, forcing, ghost_low, ghost_high)
        lower_levels = jnp.concatenate([field[None, 0, :], lower_levels[:-1]], axis=0)
        upper_levels = jnp.concatenate([field[None, -1, :], upper_levels[:-1]], axis=0)
        surfaces.append(field[height // 2].astype(jnp.bfloat16))
    surface = jnp.concatenate([surface_record[0], jnp.stack(surfaces, axis=0)], axis=0)
    rate = time_rate(surface, 0)
    data = jnp.concatenate([surface, rate], axis=1)
    theta = passage.astype(jnp.float32) * (2.0 * math.pi / passage_count)
    scale = 64.0 / math.sqrt(width * cells * passes)
    radius = face_radius[half]
    angle = face_angle[half]
    axial = face_axial[half]
    stagger = face_stagger[half]
    area = face_area[half]
    per_cell = listeners.shape[1] // cells
    block = math.gcd(per_cell * lax.axis_size("cell"), 256)

    def one_block(offset):
        rows = offset * block + jnp.arange(block, dtype=jnp.int32)
        points = jnp.take(listeners, rows, axis=1)
        kernel = kernel_pair(points, theta, radius, angle, axial, stagger, area, scale)
        return lax.dot_general(
            kernel, data, (((1,), (1,)), ((), ())), preferred_element_type=jnp.float32
        )

    blocks = lax.map(
        one_block, jnp.arange(per_cell * lax.axis_size("cell") // block, dtype=jnp.int32)
    )
    share = lax.psum_scatter(
        blocks.reshape(per_cell * lax.axis_size("cell"), blocks.shape[-1]),
        "cell",
        scatter_dimension=0,
        tiled=True,
    )
    acoustic = lax.psum(share, "pass")
    labels = jnp.arange(GROUPS, dtype=jnp.int32)
    my_groups = lax.dynamic_slice_in_dim(observer_group, cell_index * per_cell, per_cell)
    member = (my_groups[None, :] == labels[:, None]).astype(jnp.float32)
    counts = jnp.sum((observer_group[None, :] == labels[:, None]).astype(jnp.float32), axis=1)
    partial_totals = jnp.dot(
        member, acoustic, precision=lax.Precision.HIGHEST, preferred_element_type=jnp.float32
    )
    totals = lax.psum(partial_totals, "cell")
    array_signal = totals / jnp.maximum(counts, 1.0)[:, None]
    return (field, acoustic, array_signal)


def solution(mesh):
    return jax.shard_map(
        on_device,
        mesh=mesh,
        in_specs=(
            P("pass", "cell"),
            P(None, "pass", "cell"),
            P("pass", "cell"),
            P("pass", None, "cell"),
            P(),
            P("pass", "cell"),
            P("pass", None, "cell"),
            P(None, "cell"),
            P(None, "cell"),
            P(None, "cell"),
            P(None, "cell"),
            P(None, "cell"),
            P(),
            P(),
        ),
        out_specs=(P("pass", "cell"), P("cell", None), P()),
        check_vma=False,
    )
```

profile of v0, /device:TPU:0, one launch (start us, length us, event | category | flops | bytes accessed | tf_op | source)
XLA Modules:
  0.0 348.3 jit_solution(7912482702422968674)
XLA Ops:
  8.5 2.4 collective-permute-start.2
  16.5 2.4 collective-permute-start
  18.9 3.1 collective-permute-start.1
  22.1 3.2 fusion.109
  25.3 1.7 fusion.108
  28.6 4.5 %gather_fusion.1 = f32[1024]{0:T(1024)S(1)} fusion(f32[1024]{0:T(1024)S(1)} %broadcast_select_fusion.7, s32[1024]{0:T(1024)S(1)} %fusion.82), kind=kCustom, calls=%fused_computation.clone | custom fusion | bytes 12288 | tf_op jit(solution)/shard_map/jit(_take)/gather | solution.py:121
  33.2 5.1 %fusion.22 = (f32[256,1024]{1,0:T(8,128)S(1)}, f32[256,1024]{1,0:T(8,128)S(1)}) fusion(f32[256,1024]{1,0:T(8,128)S(1)} %copy-done, f32[255,1024]{1,0:T(8,128)} %get-tuple-element.332, f32[1,1024]{1,0:T(1,128)S(1)} %bitcast.169, f32[1,1024]{1,0:T(1,128)S(1)} %bitcast.172, f32[255,1024]{1,0:T(8,128)} %get-tuple-element.331, ...), kind=kLoop, calls=%fused_computation.51 | loop fusion | flops 4718592 | bytes 12582912 | tf_op jit(solution)/shard_map/add | solution.py:40
  40.0 4.0 %collective-permute-start.6 = (f32[1,256]{1,0:T(1,128)S(1)}, f32[1,256]{1,0:T(1,128)S(1)}, u32[]{:S(2)}, u32[]{:S(2)}) collective-permute-start(f32[1,256]{1,0:T(1,128)S(1)} %bitcast.206), channel_id=1, source_target_pairs={{0,1},{1,2},{2,3},{4,5},{5,6},{6,7},{8,9},{9,10},{10,11},{12,13},{... | collective-permute-start | bytes 3080 | tf_op jit(solution)/shard_map/ppermute | solution.py:19
  45.5 4.7 %collective-permute-start.5 = (f32[1024]{0:T(1024)S(1)}, f32[1024]{0:T(1024)S(1)}, u32[]{:S(2)}, u32[]{:S(2)}) collective-permute-start(f32[1024]{0:T(1024)S(1)} %bitcast.189), channel_id=1, source_target_pairs={{4,0},{8,4},{12,8},{16,12},{20,16},{24,20},{28,24},{0,28},{5,1},{9... | collective-permute-start | bytes 12296 | tf_op jit(solution)/shard_map/ppermute | solution.py:28
  50.2 1.7 fusion.105
  52.2 4.5 %gather_fusion.2 = f32[1024]{0:T(1024)S(1)} fusion(f32[1024]{0:T(1024)S(1)} %broadcast_select_fusion.6, s32[1024]{0:T(1024)S(1)} %fusion.82), kind=kCustom, calls=%fused_computation.2.clone | custom fusion | bytes 12288 | tf_op jit(solution)/shard_map/jit(_take)/gather | solution.py:121
  56.8 4.8 %fusion.27 = f32[256,1024]{1,0:T(8,128)S(1)} fusion(f32[256,1024]{1,0:T(8,128)S(1)} %copy-done, f32[255,1024]{1,0:T(8,128)} %get-tuple-element.326, f32[1,1024]{1,0:T(1,128)S(1)} %bitcast.174, f32[1,1024]{1,0:T(1,128)S(1)} %bitcast.173, f32[255,1024]{1,0:T(8,128)} %get-tuple-element.325, f32[256,1023]{1,0:T(8,128)} %get-tuple-element.324, ...), kind=kLoop, calls=%fused_computation.60 | loop fusion | flops 3670016 | bytes 12582912 | tf_op jit(solution)/shard_map/add | solution.py:40
  63.3 4.1 %collective-permute-start.10 = (f32[1,256]{1,0:T(1,128)S(1)}, f32[1,256]{1,0:T(1,128)S(1)}, u32[]{:S(2)}, u32[]{:S(2)}) collective-permute-start(f32[1,256]{1,0:T(1,128)S(1)} %bitcast.216), channel_id=1, source_target_pairs={{0,1},{1,2},{2,3},{4,5},{5,6},{6,7},{8,9},{9,10},{10,11},{12,13},{... | collective-permute-start | bytes 3080 | tf_op jit(solution)/shard_map/ppermute | solution.py:19
  68.8 4.8 %collective-permute-start.9 = (f32[1024]{0:T(1024)S(1)}, f32[1024]{0:T(1024)S(1)}, u32[]{:S(2)}, u32[]{:S(2)}) collective-permute-start(f32[1024]{0:T(1024)S(1)} %bitcast.198), channel_id=1, source_target_pairs={{4,0},{8,4},{12,8},{16,12},{20,16},{24,20},{28,24},{0,28},{5,1},{9... | collective-permute-start | bytes 12296 | tf_op jit(solution)/shard_map/ppermute | solution.py:28
  75.6 4.5 %gather_fusion.3 = f32[1024]{0:T(1024)S(1)} fusion(f32[1024]{0:T(1024)S(1)} %broadcast_select_fusion.5, s32[1024]{0:T(1024)S(1)} %fusion.82), kind=kCustom, calls=%fused_computation.3.clone | custom fusion | bytes 12288 | tf_op jit(solution)/shard_map/jit(_take)/gather | solution.py:121
  80.1 5.1 %fusion.32 = f32[256,1024]{1,0:T(8,128)S(1)} fusion(f32[256,1024]{1,0:T(8,128)S(1)} %copy-done, f32[255,1024]{1,0:T(8,128)} %get-tuple-element.320, f32[1,1024]{1,0:T(1,128)S(1)} %bitcast.176, f32[1,1024]{1,0:T(1,128)S(1)} %bitcast.175, f32[255,1024]{1,0:T(8,128)} %get-tuple-element.319, f32[256,1023]{1,0:T(8,128)} %get-tuple-element.318, ...), kind=kLoop, calls=%fused_computation.69 | loop fusion | flops 3670016 | bytes 12582912 | tf_op jit(solution)/shard_map/add | solution.py:40
  86.9 4.3 %collective-permute-start.14 = (f32[1,256]{1,0:T(1,128)S(1)}, f32[1,256]{1,0:T(1,128)S(1)}, u32[]{:S(2)}, u32[]{:S(2)}) collective-permute-start(f32[1,256]{1,0:T(1,128)S(1)} %bitcast.205), channel_id=1, source_target_pairs={{0,1},{1,2},{2,3},{4,5},{5,6},{6,7},{8,9},{9,10},{10,11},{12,13},{... | collective-permute-start | bytes 3080 | tf_op jit(solution)/shard_map/ppermute | solution.py:19
  92.6 4.7 %collective-permute-start.13 = (f32[1024]{0:T(1024)S(1)}, f32[1024]{0:T(1024)S(1)}, u32[]{:S(2)}, u32[]{:S(2)}) collective-permute-start(f32[1024]{0:T(1024)S(1)} %bitcast.190), channel_id=1, source_target_pairs={{4,0},{8,4},{12,8},{16,12},{20,16},{24,20},{28,24},{0,28},{5,1},{9... | collective-permute-start | bytes 12296 | tf_op jit(solution)/shard_map/ppermute | solution.py:28
  97.3 1.7 fusion.99
  99.4 4.5 %gather_fusion.4 = f32[1024]{0:T(1024)S(1)} fusion(f32[1024]{0:T(1024)S(1)} %broadcast_select_fusion.4, s32[1024]{0:T(1024)S(1)} %fusion.82), kind=kCustom, calls=%fused_computation.4.clone | custom fusion | bytes 12288 | tf_op jit(solution)/shard_map/jit(_take)/gather | solution.py:121
  103.9 4.8 %fusion.37 = f32[256,1024]{1,0:T(8,128)S(1)} fusion(f32[256,1024]{1,0:T(8,128)S(1)} %copy-done, f32[255,1024]{1,0:T(8,128)} %get-tuple-element.314, f32[1,1024]{1,0:T(1,128)S(1)} %bitcast.178, f32[1,1024]{1,0:T(1,128)S(1)} %bitcast.177, f32[255,1024]{1,0:T(8,128)} %get-tuple-element.313, f32[256,1023]{1,0:T(8,128)} %get-tuple-element.312, ...), kind=kLoop, calls=%fused_computation.78 | loop fusion | flops 3670016 | bytes 12582912 | tf_op jit(solution)/shard_map/add | solution.py:40
  110.4 4.4 %collective-permute-start.18 = (f32[1,256]{1,0:T(1,128)S(1)}, f32[1,256]{1,0:T(1,128)S(1)}, u32[]{:S(2)}, u32[]{:S(2)}) collective-permute-start(f32[1,256]{1,0:T(1,128)S(1)} %bitcast.217), channel_id=1, source_target_pairs={{0,1},{1,2},{2,3},{4,5},{5,6},{6,7},{8,9},{9,10},{10,11},{12,13},{... | collective-permute-start | bytes 3080 | tf_op jit(solution)/shard_map/ppermute | solution.py:19
  116.2 4.8 %collective-permute-start.17 = (f32[1024]{0:T(1024)S(1)}, f32[1024]{0:T(1024)S(1)}, u32[]{:S(2)}, u32[]{:S(2)}) collective-permute-start(f32[1024]{0:T(1024)S(1)} %bitcast.199), channel_id=1, source_target_pairs={{4,0},{8,4},{12,8},{16,12},{20,16},{24,20},{28,24},{0,28},{5,1},{9... | collective-permute-start | bytes 12296 | tf_op jit(solution)/shard_map/ppermute | solution.py:28
  123.0 4.5 %gather_fusion.5 = f32[1024]{0:T(1024)S(1)} fusion(f32[1024]{0:T(1024)S(1)} %broadcast_select_fusion.3, s32[1024]{0:T(1024)S(1)} %fusion.82), kind=kCustom, calls=%fused_computation.5.clone | custom fusion | bytes 12288 | tf_op jit(solution)/shard_map/jit(_take)/gather | solution.py:121
  127.5 5.1 %fusion.42 = f32[256,1024]{1,0:T(8,128)S(1)} fusion(f32[256,1024]{1,0:T(8,128)S(1)} %copy-done, f32[255,1024]{1,0:T(8,128)} %get-tuple-element.308, f32[1,1024]{1,0:T(1,128)S(1)} %bitcast.180, f32[1,1024]{1,0:T(1,128)S(1)} %bitcast.179, f32[255,1024]{1,0:T(8,128)} %get-tuple-element.307, f32[256,1023]{1,0:T(8,128)} %get-tuple-element.306, ...), kind=kLoop, calls=%fused_computation.87 | loop fusion | flops 3670016 | bytes 12582912 | tf_op jit(solution)/shard_map/add | solution.py:40
  134.3 4.2 %collective-permute-start.22 = (f32[1,256]{1,0:T(1,128)S(1)}, f32[1,256]{1,0:T(1,128)S(1)}, u32[]{:S(2)}, u32[]{:S(2)}) collective-permute-start(f32[1,256]{1,0:T(1,128)S(1)} %bitcast.207), channel_id=1, source_target_pairs={{0,1},{1,2},{2,3},{4,5},{5,6},{6,7},{8,9},{9,10},{10,11},{12,13},{... | collective-permute-start | bytes 3080 | tf_op jit(solution)/shard_map/ppermute | solution.py:19
  139.8 3.5 collective-permute-start.21
  143.4 1.7 fusion.93
  145.4 4.3 %collective-permute-done.20 = f32[1024]{0:T(1024)S(1)} collective-permute-done((f32[1024]{0:T(1024)S(1)}, f32[1024]{0:T(1024)S(1)}, u32[]{:S(2)}, u32[]{:S(2)}) %collective-permute-start.20) | collective-permute-done | bytes 4128 | tf_op jit(solution)/shard_map/ppermute | solution.py:28
  149.7 4.5 %gather_fusion.6 = f32[1024]{0:T(1024)S(1)} fusion(f32[1024]{0:T(1024)S(1)} %broadcast_select_fusion.2, s32[1024]{0:T(1024)S(1)} %fusion.82), kind=kCustom, calls=%fused_computation.6.clone | custom fusion | bytes 12288 | tf_op jit(solution)/shard_map/jit(_take)/gather | solution.py:121
  154.3 4.8 %fusion.47 = f32[256,1024]{1,0:T(8,128)S(1)} fusion(f32[256,1024]{1,0:T(8,128)S(1)} %copy-done, f32[255,1024]{1,0:T(8,128)} %get-tuple-element.302, f32[1,1024]{1,0:T(1,128)S(1)} %bitcast.182, f32[1,1024]{1,0:T(1,128)S(1)} %bitcast.181, f32[255,1024]{1,0:T(8,128)} %get-tuple-element.301, f32[256,1023]{1,0:T(8,128)} %get-tuple-element.300, ...), kind=kLoop, calls=%fused_computation.96 | loop fusion | flops 3670016 | bytes 12582912 | tf_op jit(solution)/shard_map/add | solution.py:40
  160.8 4.3 %collective-permute-start.26 = (f32[1,256]{1,0:T(1,128)S(1)}, f32[1,256]{1,0:T(1,128)S(1)}, u32[]{:S(2)}, u32[]{:S(2)}) collective-permute-start(f32[1,256]{1,0:T(1,128)S(1)} %bitcast.218), channel_id=1, source_target_pairs={{0,1},{1,2},{2,3},{4,5},{5,6},{6,7},{8,9},{9,10},{10,11},{12,13},{... | collective-permute-start | bytes 3080 | tf_op jit(solution)/shard_map/ppermute | solution.py:19
  166.5 4.8 %collective-permute-start.25 = (f32[1024]{0:T(1024)S(1)}, f32[1024]{0:T(1024)S(1)}, u32[]{:S(2)}, u32[]{:S(2)}) collective-permute-start(f32[1024]{0:T(1024)S(1)} %bitcast.200), channel_id=1, source_target_pairs={{4,0},{8,4},{12,8},{16,12},{20,16},{24,20},{28,24},{0,28},{5,1},{9... | collective-permute-start | bytes 12296 | tf_op jit(solution)/shard_map/ppermute | solution.py:28
  173.2 4.5 %gather_fusion.7 = f32[1024]{0:T(1024)S(1)} fusion(f32[1024]{0:T(1024)S(1)} %broadcast_select_fusion.1, s32[1024]{0:T(1024)S(1)} %fusion.82), kind=kCustom, calls=%fused_computation.7.clone | custom fusion | bytes 12288 | tf_op jit(solution)/shard_map/jit(_take)/gather | solution.py:121
  177.8 5.1 %fusion.52 = f32[256,1024]{1,0:T(8,128)S(1)} fusion(f32[256,1024]{1,0:T(8,128)S(1)} %copy-done, f32[255,1024]{1,0:T(8,128)} %get-tuple-element.296, f32[1,1024]{1,0:T(1,128)S(1)} %bitcast.184, f32[1,1024]{1,0:T(1,128)S(1)} %bitcast.183, f32[255,1024]{1,0:T(8,128)} %get-tuple-element.295, f32[256,1023]{1,0:T(8,128)} %get-tuple-element.294, ...), kind=kLoop, calls=%fused_computation.105 | loop fusion | flops 3670016 | bytes 12582912 | tf_op jit(solution)/shard_map/add | solution.py:40
  184.6 5.1 %collective-permute-start.30 = (f32[1,256]{1,0:T(1,128)S(1)}, f32[1,256]{1,0:T(1,128)S(1)}, u32[]{:S(2)}, u32[]{:S(2)}) collective-permute-start(f32[1,256]{1,0:T(1,128)S(1)} %bitcast.210), channel_id=1, source_target_pairs={{0,1},{1,2},{2,3},{4,5},{5,6},{6,7},{8,9},{9,10},{10,11},{12,13},{... | collective-permute-start | bytes 3080 | tf_op jit(solution)/shard_map/ppermute | solution.py:19
  191.2 4.7 %collective-permute-start.29 = (f32[1024]{0:T(1024)S(1)}, f32[1024]{0:T(1024)S(1)}, u32[]{:S(2)}, u32[]{:S(2)}) collective-permute-start(f32[1024]{0:T(1024)S(1)} %bitcast.188), channel_id=1, source_target_pairs={{4,0},{8,4},{12,8},{16,12},{20,16},{24,20},{28,24},{0,28},{5,1},{9... | collective-permute-start | bytes 12296 | tf_op jit(solution)/shard_map/ppermute | solution.py:28
  195.9 1.7 fusion.87
  197.9 4.5 %gather_fusion.8 = f32[1024]{0:T(1024)S(1)} fusion(f32[1024]{0:T(1024)S(1)} %broadcast_select_fusion, s32[1024]{0:T(1024)S(1)} %fusion.82), kind=kCustom, calls=%fused_computation.8.clone | custom fusion | bytes 12288 | tf_op jit(solution)/shard_map/jit(_take)/gather | solution.py:121
  202.4 4.8 %fusion.57 = f32[256,1024]{1,0:T(8,128)S(1)} fusion(f32[256,1024]{1,0:T(8,128)S(1)} %copy-done, f32[255,1024]{1,0:T(8,128)} %get-tuple-element.290, f32[1,1024]{1,0:T(1,128)S(1)} %bitcast.171, f32[1,1024]{1,0:T(1,128)S(1)} %bitcast.170, f32[255,1024]{1,0:T(8,128)} %get-tuple-element.289, f32[256,1023]{1,0:T(8,128)} %get-tuple-element.288, ...), kind=kLoop, calls=%fused_computation.114 | loop fusion | flops 3670016 | bytes 12582912 | tf_op jit(solution)/shard_map/add | solution.py:40
  209.5 23.1 %while.13 = (s32[]{:T(128)}, f32[4,256,128]{2,1,0:T(8,128)}, f32[1024]{0:T(1024)S(1)}, f32[1,1024]{1,0:T(1,128)S(1)}, f32[]{:T(128)}, /*index=5*/f32[1024]{0:T(1...) while((s32[]{:T(128)}, f32[4,256,128]{2,1,0:T(8,128)}, ...), condition=%wide.region_1.3_spmd, body=%wide.region_0.2_spmd.sunk | while | flops 141568512 | bytes 2851517 | solution.py:149
  211.0 1.8 gather_fusion
  216.7 1.8 gather_fusion
  222.5 1.8 gather_fusion
  228.3 1.8 gather_fusion
  232.9 25.6 %reduce-scatter.2.cloned.1.call-done = f32[256,128]{1,0:T(8,128)} async-done(((f32[1024,128]{1,0:T(8,128)}), f32[256,128]{1,0:T(8,128)}) %reduce-scatter.2.cloned.1.call-update) | async-done | bytes 131088 | tf_op jit(solution)/shard_map/reduce_scatter | solution.py:152
  258.5 73.9 %all-reduce.2.cloned.1.call-done = f32[256,128]{1,0:T(8,128)} async-done(((f32[256,128]{1,0:T(8,128)}), f32[256,128]{1,0:T(8,128)}) %all-reduce.2.cloned.1.call-update) | async-done | bytes 131088 | tf_op jit(solution)/shard_map/psum | solution.py:158
  333.5 5.8 %psum.15 = f32[16,128]{1,0:T(8,128)S(1)} all-reduce(f32[16,128]{1,0:T(8,128)S(1)} %fusion.66), channel_id=1, replica_groups=mesh['pass'=8,'cell'=4] {'cell'}, use_global_device_ids=true, to_apply=%region_4.6 | all-reduce | flops 2048 | bytes 16384 | tf_op jit(solution)/shard_map/psum | solution.py:166
  (228 shorter events, 54.9 us)
Async XLA Ops:
  7.2 18.1 %copy-start.4 = (f32[256,1024]{1,0:T(8,128)S(1)}, f32[256,1024]{1,0:T(8,128)}, u32[]{:S(2)}) copy-start(f32[256,1024]{1,0:T(8,128)} %param.18) | copy-start | bytes 3145732
  7.2 251.3 %reduce-scatter.2.cloned.1.call-start = ((), (), s32[]{:S(2)}) async-start(), calls=%async_computation.1 | async-start | bytes 655360 | tf_op jit(solution)/shard_map/reduce_scatter | solution.py:152
  8.5 20.0 %collective-permute-start.2 = (f32[1,256]{1,0:T(1,128)S(1)}, f32[1,256]{1,0:T(1,128)S(1)}, u32[]{:S(2)}, u32[]{:S(2)}) collective-permute-start(f32[1,256]{1,0:T(1,128)S(1)} %bitcast.202), channel_id=1, source_target_pairs={{0,1},{1,2},{2,3},{4,5},{5,6},{6,7},{8,9},{9,10},{10,11},{12,13},{... | collective-permute-start | bytes 3080 | tf_op jit(solution)/shard_map/ppermute | solution.py:19
  10.9 17.4 %collective-permute-start.3 = (f32[1,256]{1,0:T(1,128)S(1)}, f32[1,256]{1,0:T(1,128)S(1)}, u32[]{:S(2)}, u32[]{:S(2)}) collective-permute-start(f32[1,256]{1,0:T(1,128)S(1)} %bitcast.203), channel_id=1, source_target_pairs={{1,0},{2,1},{3,2},{5,4},{6,5},{7,6},{9,8},{10,9},{11,10},{13,12},{... | collective-permute-start | bytes 3080 | tf_op jit(solution)/shard_map/ppermute | solution.py:20
  16.5 12.0 %collective-permute-start = (f32[1024]{0:T(1024)S(1)}, f32[1024]{0:T(1024)S(1)}, u32[]{:S(2)}, u32[]{:S(2)}) collective-permute-start(f32[1024]{0:T(1024)S(1)} %bitcast.186), channel_id=1, source_target_pairs={{28,0},{0,4},{4,8},{8,12},{12,16},{16,20},{20,24},{24,28},{29,1},{... | collective-permute-start | bytes 12296 | tf_op jit(solution)/shard_map/ppermute | solution.py:28
  18.9 9.7 %collective-permute-start.1 = (f32[1024]{0:T(1024)S(1)}, f32[1024]{0:T(1024)S(1)}, u32[]{:S(2)}, u32[]{:S(2)}) collective-permute-start(f32[1024]{0:T(1024)S(1)} %bitcast.185), channel_id=1, source_target_pairs={{4,0},{8,4},{12,8},{16,12},{20,16},{24,20},{28,24},{0,28},{5,1},{9... | collective-permute-start | bytes 12296 | tf_op jit(solution)/shard_map/ppermute | solution.py:28
  22.0 5.0 %copy-start.9 = (s32[1,1024]{1,0:T(1,128)S(1)}, s32[1,1024]{1,0:T(1,128)}, u32[]{:S(2)}) copy-start(s32[1,1024]{1,0:T(1,128)} %param.23) | copy-start | bytes 12292
  22.0 5.0 %copy-start.10 = (f32[2,1024]{1,0:T(2,128)S(1)}, f32[2,1024]{1,0:T(2,128)}, u32[]{:S(2)}) copy-start(f32[2,1024]{1,0:T(2,128)} %param.28) | copy-start | bytes 24580
  22.0 5.1 %copy-start.11 = (f32[2,1024]{1,0:T(2,128)S(1)}, f32[2,1024]{1,0:T(2,128)}, u32[]{:S(2)}) copy-start(f32[2,1024]{1,0:T(2,128)} %param.27) | copy-start | bytes 24580
  22.0 5.1 %copy-start.12 = (f32[2,1024]{1,0:T(2,128)S(1)}, f32[2,1024]{1,0:T(2,128)}, u32[]{:S(2)}) copy-start(f32[2,1024]{1,0:T(2,128)} %param.25) | copy-start | bytes 24580
  22.0 5.2 %copy-start.13 = (f32[2,1024]{1,0:T(2,128)S(1)}, f32[2,1024]{1,0:T(2,128)}, u32[]{:S(2)}) copy-start(f32[2,1024]{1,0:T(2,128)} %param.26) | copy-start | bytes 24580
  22.0 5.2 %copy-start.14 = (f32[2,1024]{1,0:T(2,128)S(1)}, f32[2,1024]{1,0:T(2,128)}, u32[]{:S(2)}) copy-start(f32[2,1024]{1,0:T(2,128)} %param.29) | copy-start | bytes 24580
  22.0 5.2 %copy-start.7 = (f32[3,1024]{1,0:T(4,128)S(1)}, f32[3,1024]{1,0:T(4,128)}, u32[]{:S(2)}) copy-start(f32[3,1024]{1,0:T(4,128)} %param.30) | copy-start | bytes 36868
  25.3 7.9 %copy-start = (f32[256,1024]{1,0:T(8,128)S(1)}, f32[256,1024]{1,0:T(8,128)}, u32[]{:S(2)}) copy-start(f32[256,1024]{1,0:T(8,128)} %param.20) | copy-start | bytes 3145732
  38.3 7.1 %copy-start.6 = (f32[1,8,1024]{2,1,0:T(8,128)S(1)}, f32[1,8,1024]{2,1,0:T(8,128)}, u32[]{:S(2)}) copy-start(f32[1,8,1024]{2,1,0:T(8,128)} %param.21) | copy-start | bytes 98308
  40.0 12.1 %collective-permute-start.6 = (f32[1,256]{1,0:T(1,128)S(1)}, f32[1,256]{1,0:T(1,128)S(1)}, u32[]{:S(2)}, u32[]{:S(2)}) collective-permute-start(f32[1,256]{1,0:T(1,128)S(1)} %bitcast.206), channel_id=1, source_target_pairs={{0,1},{1,2},{2,3},{4,5},{5,6},{6,7},{8,9},{9,10},{10,11},{12,13},{... | collective-permute-start | bytes 3080 | tf_op jit(solution)/shard_map/ppermute | solution.py:19
  44.0 7.9 %collective-permute-start.7 = (f32[1,256]{1,0:T(1,128)S(1)}, f32[1,256]{1,0:T(1,128)S(1)}, u32[]{:S(2)}, u32[]{:S(2)}) collective-permute-start(f32[1,256]{1,0:T(1,128)S(1)} %bitcast.211), channel_id=1, source_target_pairs={{1,0},{2,1},{3,2},{5,4},{6,5},{7,6},{9,8},{10,9},{11,10},{13,12},{... | collective-permute-start | bytes 3080 | tf_op jit(solution)/shard_map/ppermute | solution.py:20
  45.4 6.8 %collective-permute-start.4 = (f32[1024]{0:T(1024)S(1)}, f32[1024]{0:T(1024)S(1)}, u32[]{:S(2)}, u32[]{:S(2)}) collective-permute-start(f32[1024]{0:T(1024)S(1)} %bitcast.192), channel_id=1, source_target_pairs={{28,0},{0,4},{4,8},{8,12},{12,16},{16,20},{20,24},{24,28},{29,1},{... | collective-permute-start | bytes 12296 | tf_op jit(solution)/shard_map/ppermute | solution.py:28
  45.5 6.7 %collective-permute-start.5 = (f32[1024]{0:T(1024)S(1)}, f32[1024]{0:T(1024)S(1)}, u32[]{:S(2)}, u32[]{:S(2)}) collective-permute-start(f32[1024]{0:T(1024)S(1)} %bitcast.189), channel_id=1, source_target_pairs={{4,0},{8,4},{12,8},{16,12},{20,16},{24,20},{28,24},{0,28},{5,1},{9... | collective-permute-start | bytes 12296 | tf_op jit(solution)/shard_map/ppermute | solution.py:28
  61.6 13.7 %copy-start.1 = (f32[256,1024]{1,0:T(8,128)}, f32[256,1024]{1,0:T(8,128)S(1)}, u32[]{:S(2)}) copy-start(f32[256,1024]{1,0:T(8,128)S(1)} %fusion.27) | copy-start | bytes 3145732
  63.3 12.1 %collective-permute-start.10 = (f32[1,256]{1,0:T(1,128)S(1)}, f32[1,256]{1,0:T(1,128)S(1)}, u32[]{:S(2)}, u32[]{:S(2)}) collective-permute-start(f32[1,256]{1,0:T(1,128)S(1)} %bitcast.216), channel_id=1, source_target_pairs={{0,1},{1,2},{2,3},{4,5},{5,6},{6,7},{8,9},{9,10},{10,11},{12,13},{... | collective-permute-start | bytes 3080 | tf_op jit(solution)/shard_map/ppermute | solution.py:19
  67.4 7.9 %collective-permute-start.11 = (f32[1,256]{1,0:T(1,128)S(1)}, f32[1,256]{1,0:T(1,128)S(1)}, u32[]{:S(2)}, u32[]{:S(2)}) collective-permute-start(f32[1,256]{1,0:T(1,128)S(1)} %bitcast.222), channel_id=1, source_target_pairs={{1,0},{2,1},{3,2},{5,4},{6,5},{7,6},{9,8},{10,9},{11,10},{13,12},{... | collective-permute-start | bytes 3080 | tf_op jit(solution)/shard_map/ppermute | solution.py:20
  68.7 6.8 %collective-permute-start.8 = (f32[1024]{0:T(1024)S(1)}, f32[1024]{0:T(1024)S(1)}, u32[]{:S(2)}, u32[]{:S(2)}) collective-permute-start(f32[1024]{0:T(1024)S(1)} %bitcast.195), channel_id=1, source_target_pairs={{28,0},{0,4},{4,8},{8,12},{12,16},{16,20},{20,24},{24,28},{29,1},{... | collective-permute-start | bytes 12296 | tf_op jit(solution)/shard_map/ppermute | solution.py:28
  68.8 6.7 %collective-permute-start.9 = (f32[1024]{0:T(1024)S(1)}, f32[1024]{0:T(1024)S(1)}, u32[]{:S(2)}, u32[]{:S(2)}) collective-permute-start(f32[1024]{0:T(1024)S(1)} %bitcast.198), channel_id=1, source_target_pairs={{4,0},{8,4},{12,8},{16,12},{20,16},{24,20},{28,24},{0,28},{5,1},{9... | collective-permute-start | bytes 12296 | tf_op jit(solution)/shard_map/ppermute | solution.py:28
  86.9 12.3 %collective-permute-start.14 = (f32[1,256]{1,0:T(1,128)S(1)}, f32[1,256]{1,0:T(1,128)S(1)}, u32[]{:S(2)}, u32[]{:S(2)}) collective-permute-start(f32[1,256]{1,0:T(1,128)S(1)} %bitcast.205), channel_id=1, source_target_pairs={{0,1},{1,2},{2,3},{4,5},{5,6},{6,7},{8,9},{9,10},{10,11},{12,13},{... | collective-permute-start | bytes 3080 | tf_op jit(solution)/shard_map/ppermute | solution.py:19
  91.2 7.9 %collective-permute-start.15 = (f32[1,256]{1,0:T(1,128)S(1)}, f32[1,256]{1,0:T(1,128)S(1)}, u32[]{:S(2)}, u32[]{:S(2)}) collective-permute-start(f32[1,256]{1,0:T(1,128)S(1)} %bitcast.208), channel_id=1, source_target_pairs={{1,0},{2,1},{3,2},{5,4},{6,5},{7,6},{9,8},{10,9},{11,10},{13,12},{... | collective-permute-start | bytes 3080 | tf_op jit(solution)/shard_map/ppermute | solution.py:20
  92.6 6.8 %collective-permute-start.12 = (f32[1024]{0:T(1024)S(1)}, f32[1024]{0:T(1024)S(1)}, u32[]{:S(2)}, u32[]{:S(2)}) collective-permute-start(f32[1024]{0:T(1024)S(1)} %bitcast.193), channel_id=1, source_target_pairs={{28,0},{0,4},{4,8},{8,12},{12,16},{16,20},{20,24},{24,28},{29,1},{... | collective-permute-start | bytes 12296 | tf_op jit(solution)/shard_map/ppermute | solution.py:28
  92.6 6.7 %collective-permute-start.13 = (f32[1024]{0:T(1024)S(1)}, f32[1024]{0:T(1024)S(1)}, u32[]{:S(2)}, u32[]{:S(2)}) collective-permute-start(f32[1024]{0:T(1024)S(1)} %bitcast.190), channel_id=1, source_target_pairs={{4,0},{8,4},{12,8},{16,12},{20,16},{24,20},{28,24},{0,28},{5,1},{9... | collective-permute-start | bytes 12296 | tf_op jit(solution)/shard_map/ppermute | solution.py:28
  108.7 13.9 %copy-start.2 = (f32[256,1024]{1,0:T(8,128)}, f32[256,1024]{1,0:T(8,128)S(1)}, u32[]{:S(2)}) copy-start(f32[256,1024]{1,0:T(8,128)S(1)} %fusion.37) | copy-start | bytes 3145732
  110.4 12.4 %collective-permute-start.18 = (f32[1,256]{1,0:T(1,128)S(1)}, f32[1,256]{1,0:T(1,128)S(1)}, u32[]{:S(2)}, u32[]{:S(2)}) collective-permute-start(f32[1,256]{1,0:T(1,128)S(1)} %bitcast.217), channel_id=1, source_target_pairs={{0,1},{1,2},{2,3},{4,5},{5,6},{6,7},{8,9},{9,10},{10,11},{12,13},{... | collective-permute-start | bytes 3080 | tf_op jit(solution)/shard_map/ppermute | solution.py:19
  114.8 7.9 %collective-permute-start.19 = (f32[1,256]{1,0:T(1,128)S(1)}, f32[1,256]{1,0:T(1,128)S(1)}, u32[]{:S(2)}, u32[]{:S(2)}) collective-permute-start(f32[1,256]{1,0:T(1,128)S(1)} %bitcast.224), channel_id=1, source_target_pairs={{1,0},{2,1},{3,2},{5,4},{6,5},{7,6},{9,8},{10,9},{11,10},{13,12},{... | collective-permute-start | bytes 3080 | tf_op jit(solution)/shard_map/ppermute | solution.py:20
  116.1 6.8 %collective-permute-start.16 = (f32[1024]{0:T(1024)S(1)}, f32[1024]{0:T(1024)S(1)}, u32[]{:S(2)}, u32[]{:S(2)}) collective-permute-start(f32[1024]{0:T(1024)S(1)} %bitcast.196), channel_id=1, source_target_pairs={{28,0},{0,4},{4,8},{8,12},{12,16},{16,20},{20,24},{24,28},{29,1},{... | collective-permute-start | bytes 12296 | tf_op jit(solution)/shard_map/ppermute | solution.py:28
  116.2 6.7 %collective-permute-start.17 = (f32[1024]{0:T(1024)S(1)}, f32[1024]{0:T(1024)S(1)}, u32[]{:S(2)}, u32[]{:S(2)}) collective-permute-start(f32[1024]{0:T(1024)S(1)} %bitcast.199), channel_id=1, source_target_pairs={{4,0},{8,4},{12,8},{16,12},{20,16},{24,20},{28,24},{0,28},{5,1},{9... | collective-permute-start | bytes 12296 | tf_op jit(solution)/shard_map/ppermute | solution.py:28
  134.3 11.0 %collective-permute-start.22 = (f32[1,256]{1,0:T(1,128)S(1)}, f32[1,256]{1,0:T(1,128)S(1)}, u32[]{:S(2)}, u32[]{:S(2)}) collective-permute-start(f32[1,256]{1,0:T(1,128)S(1)} %bitcast.207), channel_id=1, source_target_pairs={{0,1},{1,2},{2,3},{4,5},{5,6},{6,7},{8,9},{9,10},{10,11},{12,13},{... | collective-permute-start | bytes 3080 | tf_op jit(solution)/shard_map/ppermute | solution.py:19
  138.5 6.6 %collective-permute-start.23 = (f32[1,256]{1,0:T(1,128)S(1)}, f32[1,256]{1,0:T(1,128)S(1)}, u32[]{:S(2)}, u32[]{:S(2)}) collective-permute-start(f32[1,256]{1,0:T(1,128)S(1)} %bitcast.213), channel_id=1, source_target_pairs={{1,0},{2,1},{3,2},{5,4},{6,5},{7,6},{9,8},{10,9},{11,10},{13,12},{... | collective-permute-start | bytes 3080 | tf_op jit(solution)/shard_map/ppermute | solution.py:20
  139.8 5.6 %collective-permute-start.21 = (f32[1024]{0:T(1024)S(1)}, f32[1024]{0:T(1024)S(1)}, u32[]{:S(2)}, u32[]{:S(2)}) collective-permute-start(f32[1024]{0:T(1024)S(1)} %bitcast.191), channel_id=1, source_target_pairs={{4,0},{8,4},{12,8},{16,12},{20,16},{24,20},{28,24},{0,28},{5,1},{9... | collective-permute-start | bytes 12296 | tf_op jit(solution)/shard_map/ppermute | solution.py:28
  143.4 6.4 %collective-permute-start.20 = (f32[1024]{0:T(1024)S(1)}, f32[1024]{0:T(1024)S(1)}, u32[]{:S(2)}, u32[]{:S(2)}) collective-permute-start(f32[1024]{0:T(1024)S(1)} %bitcast.194), channel_id=1, source_target_pairs={{28,0},{0,4},{4,8},{8,12},{12,16},{16,20},{20,24},{24,28},{29,1},{... | collective-permute-start | bytes 12296 | tf_op jit(solution)/shard_map/ppermute | solution.py:28
  159.1 13.8 %copy-start.3 = (f32[256,1024]{1,0:T(8,128)}, f32[256,1024]{1,0:T(8,128)S(1)}, u32[]{:S(2)}) copy-start(f32[256,1024]{1,0:T(8,128)S(1)} %fusion.47) | copy-start | bytes 3145732
  160.8 12.3 %collective-permute-start.26 = (f32[1,256]{1,0:T(1,128)S(1)}, f32[1,256]{1,0:T(1,128)S(1)}, u32[]{:S(2)}, u32[]{:S(2)}) collective-permute-start(f32[1,256]{1,0:T(1,128)S(1)} %bitcast.218), channel_id=1, source_target_pairs={{0,1},{1,2},{2,3},{4,5},{5,6},{6,7},{8,9},{9,10},{10,11},{12,13},{... | collective-permute-start | bytes 3080 | tf_op jit(solution)/shard_map/ppermute | solution.py:19
  165.0 7.9 %collective-permute-start.27 = (f32[1,256]{1,0:T(1,128)S(1)}, f32[1,256]{1,0:T(1,128)S(1)}, u32[]{:S(2)}, u32[]{:S(2)}) collective-permute-start(f32[1,256]{1,0:T(1,128)S(1)} %bitcast.226), channel_id=1, source_target_pairs={{1,0},{2,1},{3,2},{5,4},{6,5},{7,6},{9,8},{10,9},{11,10},{13,12},{... | collective-permute-start | bytes 3080 | tf_op jit(solution)/shard_map/ppermute | solution.py:20
  166.4 6.8 %collective-permute-start.24 = (f32[1024]{0:T(1024)S(1)}, f32[1024]{0:T(1024)S(1)}, u32[]{:S(2)}, u32[]{:S(2)}) collective-permute-start(f32[1024]{0:T(1024)S(1)} %bitcast.197), channel_id=1, source_target_pairs={{28,0},{0,4},{4,8},{8,12},{12,16},{16,20},{20,24},{24,28},{29,1},{... | collective-permute-start | bytes 12296 | tf_op jit(solution)/shard_map/ppermute | solution.py:28
  166.5 6.7 %collective-permute-start.25 = (f32[1024]{0:T(1024)S(1)}, f32[1024]{0:T(1024)S(1)}, u32[]{:S(2)}, u32[]{:S(2)}) collective-permute-start(f32[1024]{0:T(1024)S(1)} %bitcast.200), channel_id=1, source_target_pairs={{4,0},{8,4},{12,8},{16,12},{20,16},{24,20},{28,24},{0,28},{5,1},{9... | collective-permute-start | bytes 12296 | tf_op jit(solution)/shard_map/ppermute | solution.py:28
  184.6 13.0 %collective-permute-start.30 = (f32[1,256]{1,0:T(1,128)S(1)}, f32[1,256]{1,0:T(1,128)S(1)}, u32[]{:S(2)}, u32[]{:S(2)}) collective-permute-start(f32[1,256]{1,0:T(1,128)S(1)} %bitcast.210), channel_id=1, source_target_pairs={{0,1},{1,2},{2,3},{4,5},{5,6},{6,7},{8,9},{9,10},{10,11},{12,13},{... | collective-permute-start | bytes 3080 | tf_op jit(solution)/shard_map/ppermute | solution.py:19
  189.8 7.7 %collective-permute-start.31 = (f32[1,256]{1,0:T(1,128)S(1)}, f32[1,256]{1,0:T(1,128)S(1)}, u32[]{:S(2)}, u32[]{:S(2)}) collective-permute-start(f32[1,256]{1,0:T(1,128)S(1)} %bitcast.215), channel_id=1, source_target_pairs={{1,0},{2,1},{3,2},{5,4},{6,5},{7,6},{9,8},{10,9},{11,10},{13,12},{... | collective-permute-start | bytes 3080 | tf_op jit(solution)/shard_map/ppermute | solution.py:20
  191.1 6.7 %collective-permute-start.28 = (f32[1024]{0:T(1024)S(1)}, f32[1024]{0:T(1024)S(1)}, u32[]{:S(2)}, u32[]{:S(2)}) collective-permute-start(f32[1024]{0:T(1024)S(1)} %bitcast.187), channel_id=1, source_target_pairs={{28,0},{0,4},{4,8},{8,12},{12,16},{16,20},{20,24},{24,28},{29,1},{... | collective-permute-start | bytes 12296 | tf_op jit(solution)/shard_map/ppermute | solution.py:28
  191.2 6.7 %collective-permute-start.29 = (f32[1024]{0:T(1024)S(1)}, f32[1024]{0:T(1024)S(1)}, u32[]{:S(2)}, u32[]{:S(2)}) collective-permute-start(f32[1024]{0:T(1024)S(1)} %bitcast.188), channel_id=1, source_target_pairs={{4,0},{8,4},{12,8},{16,12},{20,16},{24,20},{28,24},{0,28},{5,1},{9... | collective-permute-start | bytes 12296 | tf_op jit(solution)/shard_map/ppermute | solution.py:28
  209.5 23.2 %copy-start.8 = (s32[1024]{0:T(1024)S(1)}, s32[1024]{0:T(1024)}, u32[]{:S(2)}) copy-start(s32[1024]{0:T(1024)} %param.31) | copy-start | bytes 12292
  232.7 99.7 %all-reduce.2.cloned.1.call-start = ((), (), s32[]{:S(2)}) async-start(), calls=%async_computation.2 | async-start | bytes 262144 | tf_op jit(solution)/shard_map/psum | solution.py:158
  (1 other events, 1.0 us)
Sparse Core Ops, SparseCore 0:
  232.8 25.6 reduce-scatter.1
  261.8 70.4 all-reduce.1
where the time goes:
time: 349 us; the launch traced here: 348 us
  waiting for transfers between devices  104 us (30%)
  local copies, waits for them, and re-layouts  85.8 us (25%)
  starting transfers between devices  80.9 us (23%)
  other arithmetic  47.1 us (13%)
  between operations  16.7 us (5%)
  blocking collectives  5.77 us (2%)
  matrix products  5.43 us (2%)
    psum x1, waiting for transfers between devices, on_device(): acoustic = lax.psum(share, 'pass')  73.9 us
    add x8, other arithmetic, relax(): keep * field + coeff[0] * below + coeff[1] * above + coeff[2] * left  39.5 us
    ppermute x16, starting transfers between devices, shifted(): return lax.ppermute(block, axis, route)  37.7 us
    gather x8, local copies, waits for them, and re-layouts, on_device(): mapped = jnp.take(jnp.where(half == 0, raw_low, raw_high), local_map)  36.2 us
    ppermute x8, starting transfers between devices, padded(): before = lax.ppermute(last, axis, up)  32.7 us
    reduce_scatter x1, waiting for transfers between devices, on_device(): lax.psum_scatter(blocks.reshape(per_cell * lax.axis_size('cell'), blocks....  25.6 us
    slice x8, local copies, waits for them, and re-layouts, relax(): above = jnp.concatenate([field[1:, :], ghost_high[None, :]], axis=0)  13.6 us
    slice x8, local copies, waits for them, and re-layouts, relax(): right = jnp.concatenate([field[:, 1:], rim[3][:, None]], axis=1)  13.3 us
  transfers between devices with their start and end apart: 34, of which 3 were waited for; matrix products, arithmetic and copies ran while one was open for 7% of the time, Pallas kernels for 0%

commit v1 on v0

--- a/solution.py
+++ b/solution.py
@@ -155,7 +155,9 @@
         scatter_dimension=0,
         tiled=True,
     )
-    acoustic = lax.psum(share, "pass")
+    acoustic = share
+    for hop in (1, 2, 4):
+        acoustic = acoustic + lax.ppermute(acoustic, "pass", [(dev, dev ^ hop) for dev in range(8)])
     labels = jnp.arange(GROUPS, dtype=jnp.int32)
     my_groups = lax.dynamic_slice_in_dim(observer_group, cell_index * per_cell, per_cell)
     member = (my_groups[None, :] == labels[:, None]).astype(jnp.float32)

time: 349 us -> 292 us (0.84)
  waiting for transfers between devices: 104 us -> 42.3 us
  starting transfers between devices: 80.9 us -> 86.3 us
    psum x1 -> x0, waiting for transfers between devices: 73.9 us -> none  [on_device(): acoustic = lax.psum(share, 'pass')]
    ppermute x0 -> x3, waiting for transfers between devices: none -> 12 us  [on_device(): lax.ppermute(acoustic, 'pass', [(dev, dev ^ hop) for dev in range(8)])]
    ppermute x0 -> x3, starting transfers between devices: none -> 5.45 us  [on_device(): lax.ppermute(acoustic, 'pass', [(dev, dev ^ hop) for dev in range(8)])]
  transfers between devices with their start and end apart: 34 -> 36, of which waited for: 3 -> 5; matrix products, arithmetic and copies ran while one was open for 7% -> 8% of each run, Pallas kernels for 0% -> 0%
where the time goes in v1:
time: 292 us; the launch traced here: 291 us
  starting transfers between devices  86.3 us (30%)
  local copies, waits for them, and re-layouts  83.9 us (29%)
  other arithmetic  48 us (16%)
  waiting for transfers between devices  42.3 us (14%)
  between operations  16.7 us (6%)
  blocking collectives  6.06 us (2%)
  matrix products  4.57 us (2%)
    add x8, other arithmetic, relax(): keep * field + coeff[0] * below + coeff[1] * above + coeff[2] * left  39.5 us
    ppermute x16, starting transfers between devices, shifted(): return lax.ppermute(block, axis, route)  37.8 us
    gather x8, local copies, waits for them, and re-layouts, on_device(): mapped = jnp.take(jnp.where(half == 0, raw_low, raw_high), local_map)  36.2 us
    ppermute x8, starting transfers between devices, padded(): before = lax.ppermute(last, axis, up)  32.7 us
    reduce_scatter x1, waiting for transfers between devices, on_device(): lax.psum_scatter(blocks.reshape(per_cell * lax.axis_size('cell'), blocks....  25.9 us
    slice x8, local copies, waits for them, and re-layouts, relax(): above = jnp.concatenate([field[1:, :], ghost_high[None, :]], axis=0)  13.6 us
    slice x8, local copies, waits for them, and re-layouts, relax(): right = jnp.concatenate([field[:, 1:], rim[3][:, None]], axis=1)  13.2 us
    ppermute x3, waiting for transfers between devices, on_device(): lax.ppermute(acoustic, 'pass', [(dev, dev ^ hop) for dev in range(8)])  12 us
  transfers between devices with their start and end apart: 36, of which 5 were waited for; matrix products, arithmetic and copies ran while one was open for 8% of the time, Pallas kernels for 0%

profile of v1, /device:TPU:0, one launch (start us, length us, event | category | flops | bytes accessed | tf_op | source)
XLA Modules:
  0.0 290.5 jit_solution(13466452393940864646)
XLA Ops:
  8.5 2.4 collective-permute-start.2
  16.5 2.4 collective-permute-start
  18.9 3.1 %collective-permute-start.1 = (f32[1024]{0:T(1024)S(1)}, f32[1024]{0:T(1024)S(1)}, u32[]{:S(2)}, u32[]{:S(2)}) collective-permute-start(f32[1024]{0:T(1024)S(1)} %bitcast.185), channel_id=1, source_target_pairs={{4,0},{8,4},{12,8},{16,12},{20,16},{24,20},{28,24},{0,28},{5,1},{9... | collective-permute-start | bytes 12296 | tf_op jit(solution)/shard_map/ppermute | solution.py:28
  22.1 3.2 %fusion.109 = (f32[255,1024]{1,0:T(8,128)}, f32[255,1024]{1,0:T(8,128)}) fusion(f32[256,1024]{1,0:T(8,128)} %param.18), kind=kLoop, calls=%fused_computation.273 | loop fusion | bytes 4177920 | tf_op jit(solution)/shard_map/slice | solution.py:35
  25.3 1.7 fusion.108
  28.6 4.5 %gather_fusion.1 = f32[1024]{0:T(1024)S(1)} fusion(f32[1024]{0:T(1024)S(1)} %broadcast_select_fusion.7, s32[1024]{0:T(1024)S(1)} %fusion.82), kind=kCustom, calls=%fused_computation.clone | custom fusion | bytes 12288 | tf_op jit(solution)/shard_map/jit(_take)/gather | solution.py:121
  33.2 5.1 %fusion.22 = (f32[256,1024]{1,0:T(8,128)S(1)}, f32[256,1024]{1,0:T(8,128)S(1)}) fusion(f32[256,1024]{1,0:T(8,128)S(1)} %copy-done, f32[255,1024]{1,0:T(8,128)} %get-tuple-element.332, f32[1,1024]{1,0:T(1,128)S(1)} %bitcast.169, f32[1,1024]{1,0:T(1,128)S(1)} %bitcast.172, f32[255,1024]{1,0:T(8,128)} %get-tuple-element.331, ...), kind=kLoop, calls=%fused_computation.51 | loop fusion | flops 4718592 | bytes 12582912 | tf_op jit(solution)/shard_map/add | solution.py:40
  39.9 4.0 %collective-permute-start.6 = (f32[1,256]{1,0:T(1,128)S(1)}, f32[1,256]{1,0:T(1,128)S(1)}, u32[]{:S(2)}, u32[]{:S(2)}) collective-permute-start(f32[1,256]{1,0:T(1,128)S(1)} %bitcast.206), channel_id=1, source_target_pairs={{0,1},{1,2},{2,3},{4,5},{5,6},{6,7},{8,9},{9,10},{10,11},{12,13},{... | collective-permute-start | bytes 3080 | tf_op jit(solution)/shard_map/ppermute | solution.py:19
  45.4 4.7 %collective-permute-start.5 = (f32[1024]{0:T(1024)S(1)}, f32[1024]{0:T(1024)S(1)}, u32[]{:S(2)}, u32[]{:S(2)}) collective-permute-start(f32[1024]{0:T(1024)S(1)} %bitcast.189), channel_id=1, source_target_pairs={{4,0},{8,4},{12,8},{16,12},{20,16},{24,20},{28,24},{0,28},{5,1},{9... | collective-permute-start | bytes 12296 | tf_op jit(solution)/shard_map/ppermute | solution.py:28
  52.2 4.5 %gather_fusion.2 = f32[1024]{0:T(1024)S(1)} fusion(f32[1024]{0:T(1024)S(1)} %broadcast_select_fusion.6, s32[1024]{0:T(1024)S(1)} %fusion.82), kind=kCustom, calls=%fused_computation.2.clone | custom fusion | bytes 12288 | tf_op jit(solution)/shard_map/jit(_take)/gather | solution.py:121
  56.7 4.8 %fusion.27 = f32[256,1024]{1,0:T(8,128)S(1)} fusion(f32[256,1024]{1,0:T(8,128)S(1)} %copy-done, f32[255,1024]{1,0:T(8,128)} %get-tuple-element.326, f32[1,1024]{1,0:T(1,128)S(1)} %bitcast.174, f32[1,1024]{1,0:T(1,128)S(1)} %bitcast.173, f32[255,1024]{1,0:T(8,128)} %get-tuple-element.325, f32[256,1023]{1,0:T(8,128)} %get-tuple-element.324, ...), kind=kLoop, calls=%fused_computation.60 | loop fusion | flops 3670016 | bytes 12582912 | tf_op jit(solution)/shard_map/add | solution.py:40
  63.2 4.1 %collective-permute-start.10 = (f32[1,256]{1,0:T(1,128)S(1)}, f32[1,256]{1,0:T(1,128)S(1)}, u32[]{:S(2)}, u32[]{:S(2)}) collective-permute-start(f32[1,256]{1,0:T(1,128)S(1)} %bitcast.216), channel_id=1, source_target_pairs={{0,1},{1,2},{2,3},{4,5},{5,6},{6,7},{8,9},{9,10},{10,11},{12,13},{... | collective-permute-start | bytes 3080 | tf_op jit(solution)/shard_map/ppermute | solution.py:19
  68.8 4.8 %collective-permute-start.9 = (f32[1024]{0:T(1024)S(1)}, f32[1024]{0:T(1024)S(1)}, u32[]{:S(2)}, u32[]{:S(2)}) collective-permute-start(f32[1024]{0:T(1024)S(1)} %bitcast.198), channel_id=1, source_target_pairs={{4,0},{8,4},{12,8},{16,12},{20,16},{24,20},{28,24},{0,28},{5,1},{9... | collective-permute-start | bytes 12296 | tf_op jit(solution)/shard_map/ppermute | solution.py:28
  75.5 4.5 %gather_fusion.3 = f32[1024]{0:T(1024)S(1)} fusion(f32[1024]{0:T(1024)S(1)} %broadcast_select_fusion.5, s32[1024]{0:T(1024)S(1)} %fusion.82), kind=kCustom, calls=%fused_computation.3.clone | custom fusion | bytes 12288 | tf_op jit(solution)/shard_map/jit(_take)/gather | solution.py:121
  80.1 5.1 %fusion.32 = f32[256,1024]{1,0:T(8,128)S(1)} fusion(f32[256,1024]{1,0:T(8,128)S(1)} %copy-done, f32[255,1024]{1,0:T(8,128)} %get-tuple-element.320, f32[1,1024]{1,0:T(1,128)S(1)} %bitcast.176, f32[1,1024]{1,0:T(1,128)S(1)} %bitcast.175, f32[255,1024]{1,0:T(8,128)} %get-tuple-element.319, f32[256,1023]{1,0:T(8,128)} %get-tuple-element.318, ...), kind=kLoop, calls=%fused_computation.69 | loop fusion | flops 3670016 | bytes 12582912 | tf_op jit(solution)/shard_map/add | solution.py:40
  86.9 4.3 %collective-permute-start.14 = (f32[1,256]{1,0:T(1,128)S(1)}, f32[1,256]{1,0:T(1,128)S(1)}, u32[]{:S(2)}, u32[]{:S(2)}) collective-permute-start(f32[1,256]{1,0:T(1,128)S(1)} %bitcast.205), channel_id=1, source_target_pairs={{0,1},{1,2},{2,3},{4,5},{5,6},{6,7},{8,9},{9,10},{10,11},{12,13},{... | collective-permute-start | bytes 3080 | tf_op jit(solution)/shard_map/ppermute | solution.py:19
  92.6 4.7 %collective-permute-start.13 = (f32[1024]{0:T(1024)S(1)}, f32[1024]{0:T(1024)S(1)}, u32[]{:S(2)}, u32[]{:S(2)}) collective-permute-start(f32[1024]{0:T(1024)S(1)} %bitcast.190), channel_id=1, source_target_pairs={{4,0},{8,4},{12,8},{16,12},{20,16},{24,20},{28,24},{0,28},{5,1},{9... | collective-permute-start | bytes 12296 | tf_op jit(solution)/shard_map/ppermute | solution.py:28
  99.3 4.5 %gather_fusion.4 = f32[1024]{0:T(1024)S(1)} fusion(f32[1024]{0:T(1024)S(1)} %broadcast_select_fusion.4, s32[1024]{0:T(1024)S(1)} %fusion.82), kind=kCustom, calls=%fused_computation.4.clone | custom fusion | bytes 12288 | tf_op jit(solution)/shard_map/jit(_take)/gather | solution.py:121
  103.8 4.8 %fusion.37 = f32[256,1024]{1,0:T(8,128)S(1)} fusion(f32[256,1024]{1,0:T(8,128)S(1)} %copy-done, f32[255,1024]{1,0:T(8,128)} %get-tuple-element.314, f32[1,1024]{1,0:T(1,128)S(1)} %bitcast.178, f32[1,1024]{1,0:T(1,128)S(1)} %bitcast.177, f32[255,1024]{1,0:T(8,128)} %get-tuple-element.313, f32[256,1023]{1,0:T(8,128)} %get-tuple-element.312, ...), kind=kLoop, calls=%fused_computation.78 | loop fusion | flops 3670016 | bytes 12582912 | tf_op jit(solution)/shard_map/add | solution.py:40
  110.4 4.4 %collective-permute-start.18 = (f32[1,256]{1,0:T(1,128)S(1)}, f32[1,256]{1,0:T(1,128)S(1)}, u32[]{:S(2)}, u32[]{:S(2)}) collective-permute-start(f32[1,256]{1,0:T(1,128)S(1)} %bitcast.217), channel_id=1, source_target_pairs={{0,1},{1,2},{2,3},{4,5},{5,6},{6,7},{8,9},{9,10},{10,11},{12,13},{... | collective-permute-start | bytes 3080 | tf_op jit(solution)/shard_map/ppermute | solution.py:19
  116.2 4.8 %collective-permute-start.17 = (f32[1024]{0:T(1024)S(1)}, f32[1024]{0:T(1024)S(1)}, u32[]{:S(2)}, u32[]{:S(2)}) collective-permute-start(f32[1024]{0:T(1024)S(1)} %bitcast.199), channel_id=1, source_target_pairs={{4,0},{8,4},{12,8},{16,12},{20,16},{24,20},{28,24},{0,28},{5,1},{9... | collective-permute-start | bytes 12296 | tf_op jit(solution)/shard_map/ppermute | solution.py:28
  122.9 4.5 %gather_fusion.5 = f32[1024]{0:T(1024)S(1)} fusion(f32[1024]{0:T(1024)S(1)} %broadcast_select_fusion.3, s32[1024]{0:T(1024)S(1)} %fusion.82), kind=kCustom, calls=%fused_computation.5.clone | custom fusion | bytes 12288 | tf_op jit(solution)/shard_map/jit(_take)/gather | solution.py:121
  127.5 5.1 %fusion.42 = f32[256,1024]{1,0:T(8,128)S(1)} fusion(f32[256,1024]{1,0:T(8,128)S(1)} %copy-done, f32[255,1024]{1,0:T(8,128)} %get-tuple-element.308, f32[1,1024]{1,0:T(1,128)S(1)} %bitcast.180, f32[1,1024]{1,0:T(1,128)S(1)} %bitcast.179, f32[255,1024]{1,0:T(8,128)} %get-tuple-element.307, f32[256,1023]{1,0:T(8,128)} %get-tuple-element.306, ...), kind=kLoop, calls=%fused_computation.87 | loop fusion | flops 3670016 | bytes 12582912 | tf_op jit(solution)/shard_map/add | solution.py:40
  134.2 4.1 %collective-permute-start.22 = (f32[1,256]{1,0:T(1,128)S(1)}, f32[1,256]{1,0:T(1,128)S(1)}, u32[]{:S(2)}, u32[]{:S(2)}) collective-permute-start(f32[1,256]{1,0:T(1,128)S(1)} %bitcast.207), channel_id=1, source_target_pairs={{0,1},{1,2},{2,3},{4,5},{5,6},{6,7},{8,9},{9,10},{10,11},{12,13},{... | collective-permute-start | bytes 3080 | tf_op jit(solution)/shard_map/ppermute | solution.py:19
  139.7 3.5 %collective-permute-start.21 = (f32[1024]{0:T(1024)S(1)}, f32[1024]{0:T(1024)S(1)}, u32[]{:S(2)}, u32[]{:S(2)}) collective-permute-start(f32[1024]{0:T(1024)S(1)} %bitcast.191), channel_id=1, source_target_pairs={{4,0},{8,4},{12,8},{16,12},{20,16},{24,20},{28,24},{0,28},{5,1},{9... | collective-permute-start | bytes 12296 | tf_op jit(solution)/shard_map/ppermute | solution.py:28
  143.3 1.6 fusion.93
  145.3 4.3 %collective-permute-done.20 = f32[1024]{0:T(1024)S(1)} collective-permute-done((f32[1024]{0:T(1024)S(1)}, f32[1024]{0:T(1024)S(1)}, u32[]{:S(2)}, u32[]{:S(2)}) %collective-permute-start.20) | collective-permute-done | bytes 4128 | tf_op jit(solution)/shard_map/ppermute | solution.py:28
  149.6 4.5 %gather_fusion.6 = f32[1024]{0:T(1024)S(1)} fusion(f32[1024]{0:T(1024)S(1)} %broadcast_select_fusion.2, s32[1024]{0:T(1024)S(1)} %fusion.82), kind=kCustom, calls=%fused_computation.6.clone | custom fusion | bytes 12288 | tf_op jit(solution)/shard_map/jit(_take)/gather | solution.py:121
  154.2 4.8 %fusion.47 = f32[256,1024]{1,0:T(8,128)S(1)} fusion(f32[256,1024]{1,0:T(8,128)S(1)} %copy-done, f32[255,1024]{1,0:T(8,128)} %get-tuple-element.302, f32[1,1024]{1,0:T(1,128)S(1)} %bitcast.182, f32[1,1024]{1,0:T(1,128)S(1)} %bitcast.181, f32[255,1024]{1,0:T(8,128)} %get-tuple-element.301, f32[256,1023]{1,0:T(8,128)} %get-tuple-element.300, ...), kind=kLoop, calls=%fused_computation.96 | loop fusion | flops 3670016 | bytes 12582912 | tf_op jit(solution)/shard_map/add | solution.py:40
  160.7 4.3 %collective-permute-start.26 = (f32[1,256]{1,0:T(1,128)S(1)}, f32[1,256]{1,0:T(1,128)S(1)}, u32[]{:S(2)}, u32[]{:S(2)}) collective-permute-start(f32[1,256]{1,0:T(1,128)S(1)} %bitcast.218), channel_id=1, source_target_pairs={{0,1},{1,2},{2,3},{4,5},{5,6},{6,7},{8,9},{9,10},{10,11},{12,13},{... | collective-permute-start | bytes 3080 | tf_op jit(solution)/shard_map/ppermute | solution.py:19
  166.4 4.8 %collective-permute-start.25 = (f32[1024]{0:T(1024)S(1)}, f32[1024]{0:T(1024)S(1)}, u32[]{:S(2)}, u32[]{:S(2)}) collective-permute-start(f32[1024]{0:T(1024)S(1)} %bitcast.200), channel_id=1, source_target_pairs={{4,0},{8,4},{12,8},{16,12},{20,16},{24,20},{28,24},{0,28},{5,1},{9... | collective-permute-start | bytes 12296 | tf_op jit(solution)/shard_map/ppermute | solution.py:28
  173.1 4.5 %gather_fusion.7 = f32[1024]{0:T(1024)S(1)} fusion(f32[1024]{0:T(1024)S(1)} %broadcast_select_fusion.1, s32[1024]{0:T(1024)S(1)} %fusion.82), kind=kCustom, calls=%fused_computation.7.clone | custom fusion | bytes 12288 | tf_op jit(solution)/shard_map/jit(_take)/gather | solution.py:121
  177.7 5.1 %fusion.52 = f32[256,1024]{1,0:T(8,128)S(1)} fusion(f32[256,1024]{1,0:T(8,128)S(1)} %copy-done, f32[255,1024]{1,0:T(8,128)} %get-tuple-element.296, f32[1,1024]{1,0:T(1,128)S(1)} %bitcast.184, f32[1,1024]{1,0:T(1,128)S(1)} %bitcast.183, f32[255,1024]{1,0:T(8,128)} %get-tuple-element.295, f32[256,1023]{1,0:T(8,128)} %get-tuple-element.294, ...), kind=kLoop, calls=%fused_computation.105 | loop fusion | flops 3670016 | bytes 12582912 | tf_op jit(solution)/shard_map/add | solution.py:40
  184.6 5.1 %collective-permute-start.30 = (f32[1,256]{1,0:T(1,128)S(1)}, f32[1,256]{1,0:T(1,128)S(1)}, u32[]{:S(2)}, u32[]{:S(2)}) collective-permute-start(f32[1,256]{1,0:T(1,128)S(1)} %bitcast.210), channel_id=1, source_target_pairs={{0,1},{1,2},{2,3},{4,5},{5,6},{6,7},{8,9},{9,10},{10,11},{12,13},{... | collective-permute-start | bytes 3080 | tf_op jit(solution)/shard_map/ppermute | solution.py:19
  191.1 4.7 %collective-permute-start.29 = (f32[1024]{0:T(1024)S(1)}, f32[1024]{0:T(1024)S(1)}, u32[]{:S(2)}, u32[]{:S(2)}) collective-permute-start(f32[1024]{0:T(1024)S(1)} %bitcast.188), channel_id=1, source_target_pairs={{4,0},{8,4},{12,8},{16,12},{20,16},{24,20},{28,24},{0,28},{5,1},{9... | collective-permute-start | bytes 12296 | tf_op jit(solution)/shard_map/ppermute | solution.py:28
  197.8 4.5 %gather_fusion.8 = f32[1024]{0:T(1024)S(1)} fusion(f32[1024]{0:T(1024)S(1)} %broadcast_select_fusion, s32[1024]{0:T(1024)S(1)} %fusion.82), kind=kCustom, calls=%fused_computation.8.clone | custom fusion | bytes 12288 | tf_op jit(solution)/shard_map/jit(_take)/gather | solution.py:121
  202.3 4.8 %fusion.57 = f32[256,1024]{1,0:T(8,128)S(1)} fusion(f32[256,1024]{1,0:T(8,128)S(1)} %copy-done, f32[255,1024]{1,0:T(8,128)} %get-tuple-element.290, f32[1,1024]{1,0:T(1,128)S(1)} %bitcast.171, f32[1,1024]{1,0:T(1,128)S(1)} %bitcast.170, f32[255,1024]{1,0:T(8,128)} %get-tuple-element.289, f32[256,1023]{1,0:T(8,128)} %get-tuple-element.288, ...), kind=kLoop, calls=%fused_computation.114 | loop fusion | flops 3670016 | bytes 12582912 | tf_op jit(solution)/shard_map/add | solution.py:40
  209.4 22.8 %while.13 = (s32[]{:T(128)}, f32[4,256,128]{2,1,0:T(8,128)}, f32[1024]{0:T(1024)S(1)}, f32[1,1024]{1,0:T(1,128)S(1)}, f32[]{:T(128)}, /*index=5*/f32[1024]{0:T(1...) while((s32[]{:T(128)}, f32[4,256,128]{2,1,0:T(8,128)}, ...), condition=%wide.region_1.3_spmd, body=%wide.region_0.2_spmd.sunk | while | flops 141568512 | bytes 2851517 | solution.py:149
  210.8 1.8 gather_fusion
  216.5 1.8 gather_fusion
  222.2 1.8 gather_fusion
  227.9 1.8 gather_fusion
  232.3 25.9 %reduce-scatter.2.cloned.1.call-done = f32[256,128]{1,0:T(8,128)} async-done(((f32[1024,128]{1,0:T(8,128)}), f32[256,128]{1,0:T(8,128)}) %reduce-scatter.2.cloned.1.call-update) | async-done | bytes 131088 | tf_op jit(solution)/shard_map/reduce_scatter | solution.py:152
  259.6 3.8 %collective-permute-done.32 = f32[256,128]{1,0:T(8,128)S(1)} collective-permute-done((f32[256,128]{1,0:T(8,128)}, f32[256,128]{1,0:T(8,128)S(1)}, u32[]{:S(2)}, u32[]{:S(2)}) %collective-permute-start.32) | collective-permute-done | bytes 131104 | tf_op jit(solution)/shard_map/ppermute | solution.py:160
  266.1 3.3 %collective-permute-done.33 = f32[256,128]{1,0:T(8,128)S(1)} collective-permute-done((f32[256,128]{1,0:T(8,128)S(1)}, f32[256,128]{1,0:T(8,128)S(1)}, u32[]{:S(2)}, u32[]{:S(2)}) %collective-permute-start.33) | collective-permute-done | bytes 131104 | tf_op jit(solution)/shard_map/ppermute | solution.py:160
  269.4 2.5 collective-permute-start.34
  271.9 4.9 %collective-permute-done.34 = f32[256,128]{1,0:T(8,128)S(1)} collective-permute-done((f32[256,128]{1,0:T(8,128)S(1)}, f32[256,128]{1,0:T(8,128)S(1)}, u32[]{:S(2)}, u32[]{:S(2)}) %collective-permute-start.34) | collective-permute-done | bytes 131104 | tf_op jit(solution)/shard_map/ppermute | solution.py:160
  276.9 6.1 %psum.7 = f32[16,128]{1,0:T(8,128)S(1)} all-reduce(f32[16,128]{1,0:T(8,128)S(1)} %fusion.66), channel_id=1, replica_groups=mesh['pass'=8,'cell'=4] {'cell'}, use_global_device_ids=true, to_apply=%region_3.5 | all-reduce | flops 2048 | bytes 16384 | tf_op jit(solution)/shard_map/psum | solution.py:168
  (235 shorter events, 61.1 us)
Async XLA Ops:
  7.2 18.1 %copy-start.4 = (f32[256,1024]{1,0:T(8,128)S(1)}, f32[256,1024]{1,0:T(8,128)}, u32[]{:S(2)}) copy-start(f32[256,1024]{1,0:T(8,128)} %param.18) | copy-start | bytes 3145732
  7.2 251.0 %reduce-scatter.2.cloned.1.call-start = ((), (), s32[]{:S(2)}) async-start(), calls=%async_computation.1 | async-start | bytes 655360 | tf_op jit(solution)/shard_map/reduce_scatter | solution.py:152
  8.5 19.9 %collective-permute-start.2 = (f32[1,256]{1,0:T(1,128)S(1)}, f32[1,256]{1,0:T(1,128)S(1)}, u32[]{:S(2)}, u32[]{:S(2)}) collective-permute-start(f32[1,256]{1,0:T(1,128)S(1)} %bitcast.202), channel_id=1, source_target_pairs={{0,1},{1,2},{2,3},{4,5},{5,6},{6,7},{8,9},{9,10},{10,11},{12,13},{... | collective-permute-start | bytes 3080 | tf_op jit(solution)/shard_map/ppermute | solution.py:19
  10.9 17.4 %collective-permute-start.3 = (f32[1,256]{1,0:T(1,128)S(1)}, f32[1,256]{1,0:T(1,128)S(1)}, u32[]{:S(2)}, u32[]{:S(2)}) collective-permute-start(f32[1,256]{1,0:T(1,128)S(1)} %bitcast.203), channel_id=1, source_target_pairs={{1,0},{2,1},{3,2},{5,4},{6,5},{7,6},{9,8},{10,9},{11,10},{13,12},{... | collective-permute-start | bytes 3080 | tf_op jit(solution)/shard_map/ppermute | solution.py:20
  16.5 12.0 %collective-permute-start = (f32[1024]{0:T(1024)S(1)}, f32[1024]{0:T(1024)S(1)}, u32[]{:S(2)}, u32[]{:S(2)}) collective-permute-start(f32[1024]{0:T(1024)S(1)} %bitcast.186), channel_id=1, source_target_pairs={{28,0},{0,4},{4,8},{8,12},{12,16},{16,20},{20,24},{24,28},{29,1},{... | collective-permute-start | bytes 12296 | tf_op jit(solution)/shard_map/ppermute | solution.py:28
  18.9 9.7 %collective-permute-start.1 = (f32[1024]{0:T(1024)S(1)}, f32[1024]{0:T(1024)S(1)}, u32[]{:S(2)}, u32[]{:S(2)}) collective-permute-start(f32[1024]{0:T(1024)S(1)} %bitcast.185), channel_id=1, source_target_pairs={{4,0},{8,4},{12,8},{16,12},{20,16},{24,20},{28,24},{0,28},{5,1},{9... | collective-permute-start | bytes 12296 | tf_op jit(solution)/shard_map/ppermute | solution.py:28
  22.0 5.1 %copy-start.13 = (f32[2,1024]{1,0:T(2,128)S(1)}, f32[2,1024]{1,0:T(2,128)}, u32[]{:S(2)}) copy-start(f32[2,1024]{1,0:T(2,128)} %param.25) | copy-start | bytes 24580
  22.0 5.1 %copy-start.14 = (f32[2,1024]{1,0:T(2,128)S(1)}, f32[2,1024]{1,0:T(2,128)}, u32[]{:S(2)}) copy-start(f32[2,1024]{1,0:T(2,128)} %param.26) | copy-start | bytes 24580
  22.0 5.1 %copy-start.15 = (f32[2,1024]{1,0:T(2,128)S(1)}, f32[2,1024]{1,0:T(2,128)}, u32[]{:S(2)}) copy-start(f32[2,1024]{1,0:T(2,128)} %param.29) | copy-start | bytes 24580
  22.0 5.2 %copy-start.8 = (f32[3,1024]{1,0:T(4,128)S(1)}, f32[3,1024]{1,0:T(4,128)}, u32[]{:S(2)}) copy-start(f32[3,1024]{1,0:T(4,128)} %param.30) | copy-start | bytes 36868
  25.3 7.9 %copy-start = (f32[256,1024]{1,0:T(8,128)S(1)}, f32[256,1024]{1,0:T(8,128)}, u32[]{:S(2)}) copy-start(f32[256,1024]{1,0:T(8,128)} %param.20) | copy-start | bytes 3145732
  38.2 7.1 %copy-start.7 = (f32[1,8,1024]{2,1,0:T(8,128)S(1)}, f32[1,8,1024]{2,1,0:T(8,128)}, u32[]{:S(2)}) copy-start(f32[1,8,1024]{2,1,0:T(8,128)} %param.21) | copy-start | bytes 98308
  39.9 12.0 %collective-permute-start.6 = (f32[1,256]{1,0:T(1,128)S(1)}, f32[1,256]{1,0:T(1,128)S(1)}, u32[]{:S(2)}, u32[]{:S(2)}) collective-permute-start(f32[1,256]{1,0:T(1,128)S(1)} %bitcast.206), channel_id=1, source_target_pairs={{0,1},{1,2},{2,3},{4,5},{5,6},{6,7},{8,9},{9,10},{10,11},{12,13},{... | collective-permute-start | bytes 3080 | tf_op jit(solution)/shard_map/ppermute | solution.py:19
  44.0 7.8 %collective-permute-start.7 = (f32[1,256]{1,0:T(1,128)S(1)}, f32[1,256]{1,0:T(1,128)S(1)}, u32[]{:S(2)}, u32[]{:S(2)}) collective-permute-start(f32[1,256]{1,0:T(1,128)S(1)} %bitcast.211), channel_id=1, source_target_pairs={{1,0},{2,1},{3,2},{5,4},{6,5},{7,6},{9,8},{10,9},{11,10},{13,12},{... | collective-permute-start | bytes 3080 | tf_op jit(solution)/shard_map/ppermute | solution.py:20
  45.4 6.8 %collective-permute-start.4 = (f32[1024]{0:T(1024)S(1)}, f32[1024]{0:T(1024)S(1)}, u32[]{:S(2)}, u32[]{:S(2)}) collective-permute-start(f32[1024]{0:T(1024)S(1)} %bitcast.192), channel_id=1, source_target_pairs={{28,0},{0,4},{4,8},{8,12},{12,16},{16,20},{20,24},{24,28},{29,1},{... | collective-permute-start | bytes 12296 | tf_op jit(solution)/shard_map/ppermute | solution.py:28
  45.4 6.7 %collective-permute-start.5 = (f32[1024]{0:T(1024)S(1)}, f32[1024]{0:T(1024)S(1)}, u32[]{:S(2)}, u32[]{:S(2)}) collective-permute-start(f32[1024]{0:T(1024)S(1)} %bitcast.189), channel_id=1, source_target_pairs={{4,0},{8,4},{12,8},{16,12},{20,16},{24,20},{28,24},{0,28},{5,1},{9... | collective-permute-start | bytes 12296 | tf_op jit(solution)/shard_map/ppermute | solution.py:28
  61.5 13.7 %copy-start.1 = (f32[256,1024]{1,0:T(8,128)}, f32[256,1024]{1,0:T(8,128)S(1)}, u32[]{:S(2)}) copy-start(f32[256,1024]{1,0:T(8,128)S(1)} %fusion.27) | copy-start | bytes 3145732
  63.2 12.1 %collective-permute-start.10 = (f32[1,256]{1,0:T(1,128)S(1)}, f32[1,256]{1,0:T(1,128)S(1)}, u32[]{:S(2)}, u32[]{:S(2)}) collective-permute-start(f32[1,256]{1,0:T(1,128)S(1)} %bitcast.216), channel_id=1, source_target_pairs={{0,1},{1,2},{2,3},{4,5},{5,6},{6,7},{8,9},{9,10},{10,11},{12,13},{... | collective-permute-start | bytes 3080 | tf_op jit(solution)/shard_map/ppermute | solution.py:19
  67.3 7.8 %collective-permute-start.11 = (f32[1,256]{1,0:T(1,128)S(1)}, f32[1,256]{1,0:T(1,128)S(1)}, u32[]{:S(2)}, u32[]{:S(2)}) collective-permute-start(f32[1,256]{1,0:T(1,128)S(1)} %bitcast.222), channel_id=1, source_target_pairs={{1,0},{2,1},{3,2},{5,4},{6,5},{7,6},{9,8},{10,9},{11,10},{13,12},{... | collective-permute-start | bytes 3080 | tf_op jit(solution)/shard_map/ppermute | solution.py:20
  68.7 6.8 %collective-permute-start.8 = (f32[1024]{0:T(1024)S(1)}, f32[1024]{0:T(1024)S(1)}, u32[]{:S(2)}, u32[]{:S(2)}) collective-permute-start(f32[1024]{0:T(1024)S(1)} %bitcast.195), channel_id=1, source_target_pairs={{28,0},{0,4},{4,8},{8,12},{12,16},{16,20},{20,24},{24,28},{29,1},{... | collective-permute-start | bytes 12296 | tf_op jit(solution)/shard_map/ppermute | solution.py:28
  68.8 6.7 %collective-permute-start.9 = (f32[1024]{0:T(1024)S(1)}, f32[1024]{0:T(1024)S(1)}, u32[]{:S(2)}, u32[]{:S(2)}) collective-permute-start(f32[1024]{0:T(1024)S(1)} %bitcast.198), channel_id=1, source_target_pairs={{4,0},{8,4},{12,8},{16,12},{20,16},{24,20},{28,24},{0,28},{5,1},{9... | collective-permute-start | bytes 12296 | tf_op jit(solution)/shard_map/ppermute | solution.py:28
  86.9 12.3 %collective-permute-start.14 = (f32[1,256]{1,0:T(1,128)S(1)}, f32[1,256]{1,0:T(1,128)S(1)}, u32[]{:S(2)}, u32[]{:S(2)}) collective-permute-start(f32[1,256]{1,0:T(1,128)S(1)} %bitcast.205), channel_id=1, source_target_pairs={{0,1},{1,2},{2,3},{4,5},{5,6},{6,7},{8,9},{9,10},{10,11},{12,13},{... | collective-permute-start | bytes 3080 | tf_op jit(solution)/shard_map/ppermute | solution.py:19
  91.1 7.8 %collective-permute-start.15 = (f32[1,256]{1,0:T(1,128)S(1)}, f32[1,256]{1,0:T(1,128)S(1)}, u32[]{:S(2)}, u32[]{:S(2)}) collective-permute-start(f32[1,256]{1,0:T(1,128)S(1)} %bitcast.208), channel_id=1, source_target_pairs={{1,0},{2,1},{3,2},{5,4},{6,5},{7,6},{9,8},{10,9},{11,10},{13,12},{... | collective-permute-start | bytes 3080 | tf_op jit(solution)/shard_map/ppermute | solution.py:20
  92.5 6.8 %collective-permute-start.12 = (f32[1024]{0:T(1024)S(1)}, f32[1024]{0:T(1024)S(1)}, u32[]{:S(2)}, u32[]{:S(2)}) collective-permute-start(f32[1024]{0:T(1024)S(1)} %bitcast.193), channel_id=1, source_target_pairs={{28,0},{0,4},{4,8},{8,12},{12,16},{16,20},{20,24},{24,28},{29,1},{... | collective-permute-start | bytes 12296 | tf_op jit(solution)/shard_map/ppermute | solution.py:28
  92.6 6.7 %collective-permute-start.13 = (f32[1024]{0:T(1024)S(1)}, f32[1024]{0:T(1024)S(1)}, u32[]{:S(2)}, u32[]{:S(2)}) collective-permute-start(f32[1024]{0:T(1024)S(1)} %bitcast.190), channel_id=1, source_target_pairs={{4,0},{8,4},{12,8},{16,12},{20,16},{24,20},{28,24},{0,28},{5,1},{9... | collective-permute-start | bytes 12296 | tf_op jit(solution)/shard_map/ppermute | solution.py:28
  108.6 13.9 %copy-start.2 = (f32[256,1024]{1,0:T(8,128)}, f32[256,1024]{1,0:T(8,128)S(1)}, u32[]{:S(2)}) copy-start(f32[256,1024]{1,0:T(8,128)S(1)} %fusion.37) | copy-start | bytes 3145732
  110.4 12.4 %collective-permute-start.18 = (f32[1,256]{1,0:T(1,128)S(1)}, f32[1,256]{1,0:T(1,128)S(1)}, u32[]{:S(2)}, u32[]{:S(2)}) collective-permute-start(f32[1,256]{1,0:T(1,128)S(1)} %bitcast.217), channel_id=1, source_target_pairs={{0,1},{1,2},{2,3},{4,5},{5,6},{6,7},{8,9},{9,10},{10,11},{12,13},{... | collective-permute-start | bytes 3080 | tf_op jit(solution)/shard_map/ppermute | solution.py:19
  114.7 7.8 %collective-permute-start.19 = (f32[1,256]{1,0:T(1,128)S(1)}, f32[1,256]{1,0:T(1,128)S(1)}, u32[]{:S(2)}, u32[]{:S(2)}) collective-permute-start(f32[1,256]{1,0:T(1,128)S(1)} %bitcast.224), channel_id=1, source_target_pairs={{1,0},{2,1},{3,2},{5,4},{6,5},{7,6},{9,8},{10,9},{11,10},{13,12},{... | collective-permute-start | bytes 3080 | tf_op jit(solution)/shard_map/ppermute | solution.py:20
  116.1 6.8 %collective-permute-start.16 = (f32[1024]{0:T(1024)S(1)}, f32[1024]{0:T(1024)S(1)}, u32[]{:S(2)}, u32[]{:S(2)}) collective-permute-start(f32[1024]{0:T(1024)S(1)} %bitcast.196), channel_id=1, source_target_pairs={{28,0},{0,4},{4,8},{8,12},{12,16},{16,20},{20,24},{24,28},{29,1},{... | collective-permute-start | bytes 12296 | tf_op jit(solution)/shard_map/ppermute | solution.py:28
  116.2 6.7 %collective-permute-start.17 = (f32[1024]{0:T(1024)S(1)}, f32[1024]{0:T(1024)S(1)}, u32[]{:S(2)}, u32[]{:S(2)}) collective-permute-start(f32[1024]{0:T(1024)S(1)} %bitcast.199), channel_id=1, source_target_pairs={{4,0},{8,4},{12,8},{16,12},{20,16},{24,20},{28,24},{0,28},{5,1},{9... | collective-permute-start | bytes 12296 | tf_op jit(solution)/shard_map/ppermute | solution.py:28
  134.2 10.9 %collective-permute-start.22 = (f32[1,256]{1,0:T(1,128)S(1)}, f32[1,256]{1,0:T(1,128)S(1)}, u32[]{:S(2)}, u32[]{:S(2)}) collective-permute-start(f32[1,256]{1,0:T(1,128)S(1)} %bitcast.207), channel_id=1, source_target_pairs={{0,1},{1,2},{2,3},{4,5},{5,6},{6,7},{8,9},{9,10},{10,11},{12,13},{... | collective-permute-start | bytes 3080 | tf_op jit(solution)/shard_map/ppermute | solution.py:19
  138.4 6.6 %collective-permute-start.23 = (f32[1,256]{1,0:T(1,128)S(1)}, f32[1,256]{1,0:T(1,128)S(1)}, u32[]{:S(2)}, u32[]{:S(2)}) collective-permute-start(f32[1,256]{1,0:T(1,128)S(1)} %bitcast.213), channel_id=1, source_target_pairs={{1,0},{2,1},{3,2},{5,4},{6,5},{7,6},{9,8},{10,9},{11,10},{13,12},{... | collective-permute-start | bytes 3080 | tf_op jit(solution)/shard_map/ppermute | solution.py:20
  139.7 5.6 %collective-permute-start.21 = (f32[1024]{0:T(1024)S(1)}, f32[1024]{0:T(1024)S(1)}, u32[]{:S(2)}, u32[]{:S(2)}) collective-permute-start(f32[1024]{0:T(1024)S(1)} %bitcast.191), channel_id=1, source_target_pairs={{4,0},{8,4},{12,8},{16,12},{20,16},{24,20},{28,24},{0,28},{5,1},{9... | collective-permute-start | bytes 12296 | tf_op jit(solution)/shard_map/ppermute | solution.py:28
  143.3 6.4 %collective-permute-start.20 = (f32[1024]{0:T(1024)S(1)}, f32[1024]{0:T(1024)S(1)}, u32[]{:S(2)}, u32[]{:S(2)}) collective-permute-start(f32[1024]{0:T(1024)S(1)} %bitcast.194), channel_id=1, source_target_pairs={{28,0},{0,4},{4,8},{8,12},{12,16},{16,20},{20,24},{24,28},{29,1},{... | collective-permute-start | bytes 12296 | tf_op jit(solution)/shard_map/ppermute | solution.py:28
  159.0 13.8 %copy-start.3 = (f32[256,1024]{1,0:T(8,128)}, f32[256,1024]{1,0:T(8,128)S(1)}, u32[]{:S(2)}) copy-start(f32[256,1024]{1,0:T(8,128)S(1)} %fusion.47) | copy-start | bytes 3145732
  160.7 12.3 %collective-permute-start.26 = (f32[1,256]{1,0:T(1,128)S(1)}, f32[1,256]{1,0:T(1,128)S(1)}, u32[]{:S(2)}, u32[]{:S(2)}) collective-permute-start(f32[1,256]{1,0:T(1,128)S(1)} %bitcast.218), channel_id=1, source_target_pairs={{0,1},{1,2},{2,3},{4,5},{5,6},{6,7},{8,9},{9,10},{10,11},{12,13},{... | collective-permute-start | bytes 3080 | tf_op jit(solution)/shard_map/ppermute | solution.py:19
  165.0 7.8 %collective-permute-start.27 = (f32[1,256]{1,0:T(1,128)S(1)}, f32[1,256]{1,0:T(1,128)S(1)}, u32[]{:S(2)}, u32[]{:S(2)}) collective-permute-start(f32[1,256]{1,0:T(1,128)S(1)} %bitcast.226), channel_id=1, source_target_pairs={{1,0},{2,1},{3,2},{5,4},{6,5},{7,6},{9,8},{10,9},{11,10},{13,12},{... | collective-permute-start | bytes 3080 | tf_op jit(solution)/shard_map/ppermute | solution.py:20
  166.3 6.8 %collective-permute-start.24 = (f32[1024]{0:T(1024)S(1)}, f32[1024]{0:T(1024)S(1)}, u32[]{:S(2)}, u32[]{:S(2)}) collective-permute-start(f32[1024]{0:T(1024)S(1)} %bitcast.197), channel_id=1, source_target_pairs={{28,0},{0,4},{4,8},{8,12},{12,16},{16,20},{20,24},{24,28},{29,1},{... | collective-permute-start | bytes 12296 | tf_op jit(solution)/shard_map/ppermute | solution.py:28
  166.4 6.7 %collective-permute-start.25 = (f32[1024]{0:T(1024)S(1)}, f32[1024]{0:T(1024)S(1)}, u32[]{:S(2)}, u32[]{:S(2)}) collective-permute-start(f32[1024]{0:T(1024)S(1)} %bitcast.200), channel_id=1, source_target_pairs={{4,0},{8,4},{12,8},{16,12},{20,16},{24,20},{28,24},{0,28},{5,1},{9... | collective-permute-start | bytes 12296 | tf_op jit(solution)/shard_map/ppermute | solution.py:28
  184.6 13.0 %collective-permute-start.30 = (f32[1,256]{1,0:T(1,128)S(1)}, f32[1,256]{1,0:T(1,128)S(1)}, u32[]{:S(2)}, u32[]{:S(2)}) collective-permute-start(f32[1,256]{1,0:T(1,128)S(1)} %bitcast.210), channel_id=1, source_target_pairs={{0,1},{1,2},{2,3},{4,5},{5,6},{6,7},{8,9},{9,10},{10,11},{12,13},{... | collective-permute-start | bytes 3080 | tf_op jit(solution)/shard_map/ppermute | solution.py:19
  189.7 7.7 %collective-permute-start.31 = (f32[1,256]{1,0:T(1,128)S(1)}, f32[1,256]{1,0:T(1,128)S(1)}, u32[]{:S(2)}, u32[]{:S(2)}) collective-permute-start(f32[1,256]{1,0:T(1,128)S(1)} %bitcast.215), channel_id=1, source_target_pairs={{1,0},{2,1},{3,2},{5,4},{6,5},{7,6},{9,8},{10,9},{11,10},{13,12},{... | collective-permute-start | bytes 3080 | tf_op jit(solution)/shard_map/ppermute | solution.py:20
  191.0 6.7 %collective-permute-start.28 = (f32[1024]{0:T(1024)S(1)}, f32[1024]{0:T(1024)S(1)}, u32[]{:S(2)}, u32[]{:S(2)}) collective-permute-start(f32[1024]{0:T(1024)S(1)} %bitcast.187), channel_id=1, source_target_pairs={{28,0},{0,4},{4,8},{8,12},{12,16},{16,20},{20,24},{24,28},{29,1},{... | collective-permute-start | bytes 12296 | tf_op jit(solution)/shard_map/ppermute | solution.py:28
  191.1 6.7 %collective-permute-start.29 = (f32[1024]{0:T(1024)S(1)}, f32[1024]{0:T(1024)S(1)}, u32[]{:S(2)}, u32[]{:S(2)}) collective-permute-start(f32[1024]{0:T(1024)S(1)} %bitcast.188), channel_id=1, source_target_pairs={{4,0},{8,4},{12,8},{16,12},{20,16},{24,20},{28,24},{0,28},{5,1},{9... | collective-permute-start | bytes 12296 | tf_op jit(solution)/shard_map/ppermute | solution.py:28
  209.4 56.5 %copy-start.9 = (s32[1024]{0:T(1024)S(1)}, s32[1024]{0:T(1024)}, u32[]{:S(2)}) copy-start(s32[1024]{0:T(1024)} %param.31) | copy-start | bytes 12292
  258.1 5.3 %collective-permute-start.32 = (f32[256,128]{1,0:T(8,128)}, f32[256,128]{1,0:T(8,128)S(1)}, u32[]{:S(2)}, u32[]{:S(2)}) collective-permute-start(f32[256,128]{1,0:T(8,128)} %reduce-scatter.2.cloned.1.call-done), channel_id=1, source_target_pairs={{0,4},{4,0},{8,12},{12,8},{16,20},{20,16},{24,28},{28,24},{1,5},{5... | collective-permute-start | bytes 393224 | tf_op jit(solution)/shard_map/ppermute | solution.py:160
  264.4 5.0 %collective-permute-start.33 = (f32[256,128]{1,0:T(8,128)S(1)}, f32[256,128]{1,0:T(8,128)S(1)}, u32[]{:S(2)}, u32[]{:S(2)}) collective-permute-start(f32[256,128]{1,0:T(8,128)S(1)} %add.365), channel_id=1, source_target_pairs={{0,8},{4,12},{8,0},{12,4},{16,24},{20,28},{24,16},{28,20},{1,9},{5... | collective-permute-start | bytes 393224 | tf_op jit(solution)/shard_map/ppermute | solution.py:160
  269.4 7.3 %collective-permute-start.34 = (f32[256,128]{1,0:T(8,128)S(1)}, f32[256,128]{1,0:T(8,128)S(1)}, u32[]{:S(2)}, u32[]{:S(2)}) collective-permute-start(f32[256,128]{1,0:T(8,128)S(1)} %add.366), channel_id=1, source_target_pairs={{0,16},{4,20},{8,24},{12,28},{16,0},{20,4},{24,8},{28,12},{1,17},{... | collective-permute-start | bytes 393224 | tf_op jit(solution)/shard_map/ppermute | solution.py:160
  276.8 6.9 %copy-start.6 = (f32[256,128]{1,0:T(8,128)}, f32[256,128]{1,0:T(8,128)S(1)}, u32[]{:S(2)}) copy-start(f32[256,128]{1,0:T(8,128)S(1)} %add.367) | copy-start | bytes 393220
  (4 other events, 16.0 us)
Sparse Core Ops, SparseCore 0:
  232.4 25.7 reduce-scatter.1
